TPU v7x, 32 devices: a whole 2x2x4 slice. The times are simulated.
32 devices in a mesh: gx: 8 (over z, x), gy: 4 (over y, core).
Axes of the slice: x: 2, y: 2, z: 4, core: 2. Of those that a mesh axis runs over, the one named last changes fastest.
Arguments:
- density: float32 [512, 128, 128], P('gx', 'gy'), may hold values from -6 to 6
- slowness: float32 [512, 128, 128], P('gx', 'gy'), may hold values from -6 to 6
- pressure_obs: float32 [512, 128, 128], P('gx', 'gy'), may hold values from -6 to 6
- time_obs: float32 [512, 128, 128], P('gx', 'gy'), may hold values from -6 to 6
- zone_map: int32 [512, 128, 128], P('gx', 'gy'), may hold values from 0 to 7
- zone_low: float32 [8], replicated, may hold values from -2.5 to -0.5
- zone_high: float32 [8], replicated, may hold values from 0.5 to 2.5
Outputs:
- density_out: float32 [512, 128, 128], P('gx', 'gy')
- slowness_out: float32 [512, 128, 128], P('gx', 'gy')
- objective: float32 [3], replicated
All inputs are finite; a program needn't handle non-finite values.
Results may differ from a plain program's by a relative error of at most 0.00013.
Values sent between devices are 32-bit elements; how exact they have to be, the bound alone decides.
A program may use at most 128 MiB of HBM per device.

v0:
```python
import functools
import math

import jax
import jax.numpy as jnp
from jax import lax
from jax.experimental import pallas as pl
from jax.experimental.pallas import tpu as pltpu
from jax.sharding import PartitionSpec as P

ITERS = 3
BETA = 1.0
ETA = 0.5
EPSILON = 1e-06
MESH = pl.DeviceIdType.MESH
F32 = jnp.float32
BF16 = jnp.bfloat16


def split(v):
    hi = v.astype(BF16)
    lo = (v - hi.astype(F32)).astype(BF16)
    return jnp.concatenate([hi, lo], axis=-1)


def kernel(
    nx, ny,
    zlow, zhigh, rho_h, sig_h, p_h, t_h, zone_h,
    rho_o, sig_o, obj_o,
    rho, sig, low, high, p, t, zone, grho, gsig, gp, lin,
    u1, v1, u2, v2, e3, f3, da, db, dedge, wts, ltab,
    rim, rim2, ysend, yrecv, xrecv, csend, crecv, pwsend, pwrecv, before, zsum, nsend, nrecv,
    insem, ys, yr, xs_, xr, cs, cr, ps, pr, ns, nr,
):
    X, Y, Z = p.shape
    mx, my = lax.axis_index("gx"), lax.axis_index("gy")
    n = nx * ny
    me = mx * ny + my
    N = nx * X
    cells = float(N * ny * Y * Z)
    zscale = 1.0 / math.sqrt(Z)
    xscale = 1.0 / math.sqrt(N)
    R = pl.ds(8, Y)
    i0 = (mx * X).astype(F32)

    inner = (pl.ds(2, X), R)
    loads = [
        pltpu.make_async_copy(sig_h, sig.at[inner], insem.at[0]),
        pltpu.make_async_copy(rho_h, rho.at[inner], insem.at[1]),
        pltpu.make_async_copy(t_h, t, insem.at[2]),
        pltpu.make_async_copy(zone_h, zone, insem.at[3]),
        pltpu.make_async_copy(p_h, p, insem.at[4]),
    ]
    for c in loads:
        c.start()
    barrier = pltpu.get_barrier_semaphore()

    has = {0: (mx > 0, my > 0), 1: (mx < nx - 1, my < ny - 1)}

    def zero_y(s):
        @pl.when(jnp.logical_not(has[s][1]))
        def _():
            for r in range(4):
                yrecv[r, s] = jnp.zeros(yrecv.shape[2:], F32)

    def zero_x(s):
        @pl.when(jnp.logical_not(has[s][0]))
        def _():
            for r in range(4):
                xrecv[r, s] = jnp.zeros(xrecv.shape[2:], F32)

    for s in range(2):
        zero_y(s)
        zero_x(s)
    for sx in range(2):
        for sy in range(2):
            @pl.when(jnp.logical_not(jnp.logical_and(has[sx][0], has[sy][1])))
            def _():
                for r in range(4):
                    crecv[r, sx, sy] = jnp.zeros((8, Z), F32)
    csend[...] = jnp.zeros(csend.shape, F32)

    def others(d):
        to = lax.rem(me + d, n)
        return to, (to // ny, lax.rem(to, ny))

    def greet(d, carry):
        _, dev = others(d)
        pl.semaphore_signal(barrier, inc=1, device_id=dev, device_id_type=MESH)
        return carry

    lax.fori_loop(1, n, greet, 0)

    def ycopy(r, s):
        b = 1 if r == 3 else 0
        return pltpu.make_async_remote_copy(
            src_ref=ysend.at[b, s], dst_ref=yrecv.at[r, 1 - s],
            send_sem=ys.at[r, s], recv_sem=yr.at[r, 1 - s],
            device_id=(mx, my + (2 * s - 1)), device_id_type=MESH)

    def xsource(r, s, f):
        if r == 0:
            src = (rho, sig)[f]
            return src.at[pl.ds(2 + s * (X - 2), 2), R]
        src = ((low, high) if r == 3 else (grho, gsig))[f]
        return src.at[pl.ds(s * (X - 2), 2)]

    def xcopy(r, s, f):
        return pltpu.make_async_remote_copy(
            src_ref=xsource(r, s, f), dst_ref=xrecv.at[r, 1 - s, f],
            send_sem=xs_.at[r, s, f], recv_sem=xr.at[r, 1 - s, f],
            device_id=(mx + (2 * s - 1), my), device_id_type=MESH)

    def ccopy(r, sx, sy):
        b = 1 if r == 3 else 0
        return pltpu.make_async_remote_copy(
            src_ref=csend.at[b, sx, sy], dst_ref=crecv.at[r, 1 - sx, 1 - sy],
            send_sem=cs.at[r, sx, sy], recv_sem=cr.at[r, 1 - sx, 1 - sy],
            device_id=(mx + (2 * sx - 1), my + (2 * sy - 1)), device_id_type=MESH)

    def rims_start(r):
        for s in range(2):
            @pl.when(has[s][1])
            def _():
                ycopy(r, s).start()

            @pl.when(has[s][0])
            def _():
                for f in range(2):
                    xcopy(r, s, f).start()
        for sx in range(2):
            for sy in range(2):
                @pl.when(jnp.logical_and(has[sx][0], has[sy][1]))
                def _():
                    ccopy(r, sx, sy).start()

    def rims_wait(r):
        for s in range(2):
            @pl.when(has[s][1])
            def _():
                ycopy(r, 1 - s).wait_recv()
                ycopy(r, s).wait_send()

            @pl.when(has[s][0])
            def _():
                for f in range(2):
                    xcopy(r, 1 - s, f).wait_recv()
                    xcopy(r, s, f).wait_send()
        for sx in range(2):
            for sy in range(2):
                @pl.when(jnp.logical_and(has[sx][0], has[sy][1]))
                def _():
                    ccopy(r, 1 - sx, 1 - sy).wait_recv()
                    ccopy(r, sx, sy).wait_send()

    def pwcopy(r, tx, slot):
        later = jnp.where(tx > mx, 0, 1)
        return pltpu.make_async_remote_copy(
            src_ref=pwsend.at[later], dst_ref=pwrecv.at[r, slot],
            send_sem=ps.at[r, tx], recv_sem=pr.at[r, slot],
            device_id=(tx, my), device_id_type=MESH)

    def pw_start(r):
        def go(d, carry):
            pwcopy(r, lax.rem(mx + d, nx), mx).start()
            return carry
        lax.fori_loop(1, nx, go, 0)

    def pw_wait(r):
        def go(d, carry):
            tx = lax.rem(mx + d, nx)
            pwcopy(r, tx, tx).wait_recv()
            pwcopy(r, tx, tx).wait_send()
            return carry
        lax.fori_loop(1, nx, go, 0)

        def add(d, carry):
            a, b = carry
            tx = lax.rem(mx + d, nx)
            v = pwrecv[r, tx]
            w = jnp.where(tx < mx, 1.0, 0.0)
            return a + v * w, b + v * (1.0 - w)
        zero = jnp.zeros((Y, Z), F32)
        return lax.fori_loop(1, nx, add, (zero, zero))

    def ncopy(r, to, dev, slot):
        return pltpu.make_async_remote_copy(
            src_ref=nsend.at[r], dst_ref=nrecv.at[r, slot],
            send_sem=ns.at[to], recv_sem=nr.at[r % 2, slot],
            device_id=dev, device_id_type=MESH)

    def n_start(r):
        def go(d, carry):
            to, dev = others(d)
            ncopy(r, to, dev, me).start()
            return carry
        lax.fori_loop(1, n, go, 0)

    def n_wait(r):
        def go(d, carry):
            to, dev = others(d)
            ncopy(r, to, dev, to).wait_recv()
            ncopy(r, to, dev, to).wait_send()
            return carry
        lax.fori_loop(1, n, go, 0)
        tot = nrecv[r, 0]
        for s in range(1, n):
            tot = tot + nrecv[r, s]
        return jnp.sum(tot, axis=1, keepdims=True)

    def fold(v):
        out = v[0:8]
        for k in range(8, v.shape[0], 8):
            out = out + v[k:k + 8]
        return out

    def gather(b, f, x, v):
        row = pl.ds(x, 1)
        ysend[b, 0, f, 0, row, :] = v[0:1]
        ysend[b, 0, f, 1, row, :] = v[1:2]
        ysend[b, 1, f, 0, row, :] = v[Y - 1:Y]
        ysend[b, 1, f, 1, row, :] = v[Y - 2:Y - 1]

    def corners(b, f):
        for sx in range(2):
            for sy in range(2):
                csend[b, sx, sy, f:f + 1, :] = ysend[b, sy, f, 0, sx * (X - 1):sx * (X - 1) + 1, :]

    zero = jnp.zeros((Y, Z), F32)

    loads[0].wait()
    loads[2].wait()

    def sums(x, carry):
        a, b, c = carry
        v = sig[x + 2, R, :]
        gather(0, 1, x, v)
        weight = float(N) - i0 - x.astype(F32)
        return a + v, b + weight * v, c + t[x]

    psum_, wsum, tsum = lax.fori_loop(0, X, sums, (zero, zero, zero), unroll=4)
    zown = xscale * wsum - tsum
    pwsend[0] = psum_
    pwsend[1] = zown
    loads[1].wait()

    def copy_rho(x, carry):
        gather(0, 0, x, rho[x + 2, R, :])
        return carry

    lax.fori_loop(0, X, copy_rho, 0, unroll=4)
    corners(0, 0)
    corners(0, 1)
    pl.semaphore_wait(barrier, n - 1)
    rims_start(0)
    pw_start(0)

    loads[3].wait()

    def bounds(x, carry):
        ids = zone[x]
        lo = jnp.zeros((Y, Z), F32)
        hi = jnp.zeros((Y, Z), F32)
        for k in range(zlow.shape[0]):
            hit = ids == k
            lo = jnp.where(hit, zlow[k], lo)
            hi = jnp.where(hit, zhigh[k], hi)
        low[x] = lo
        high[x] = hi
        gather(1, 0, x, lo)
        gather(1, 1, x, hi)
        return carry

    lax.fori_loop(0, X, bounds, 0, unroll=2)
    corners(1, 0)
    corners(1, 1)
    rims_start(3)

    ri = lax.broadcasted_iota(jnp.int32, (Z, Z), 0)
    ci = lax.broadcasted_iota(jnp.int32, (Z, Z), 1)
    m = (Z - jnp.maximum(ri, ci)).astype(F32).astype(BF16)
    u = jnp.where(ri <= ci, 1.0, 0.0).astype(BF16)
    l = jnp.where(ri >= ci, 1.0, 0.0).astype(BF16)
    band = jnp.where(ri == ci + 1, 1.0, jnp.where(ri == ci - 1, -1.0, 0.0)).astype(BF16)
    for half in (slice(0, Z), slice(Z, 2 * Z)):
        wts[half, 0:Z] = m
        wts[half, Z:2 * Z] = band
        wts[half, 2 * Z:3 * Z] = u
    ltab[0:Z] = l
    ltab[Z:2 * Z] = l

    block = X
    band2 = wts.at[:, pl.ds(Z, Z)]

    def slope(v):
        return jnp.dot(split(v), band2[...], preferred_element_type=F32)

    loads[4].wait()

    def pback(k, carry):
        rows = pl.ds(k * block, block)
        v = p[rows].reshape(block * Y, Z)
        out = jnp.dot(split(v), ltab[...], preferred_element_type=F32)
        gp[rows] = (out * zscale).reshape(block, Y, Z)
        return carry

    lax.fori_loop(0, X // block, pback, 0)

    def zlin(k, carry):
        v = rho[pl.ds(2 + k * block, block), R, :].reshape(block * Y, Z)
        out = jnp.dot(split(v), wts[...], preferred_element_type=F32)
        rows = pl.ds(k * block, block)
        lin[rows] = out[:, 0:Z].reshape(block, Y, Z)
        da[rows] = out[:, Z:2 * Z].reshape(block, Y, Z)
        rp = zscale * out[:, 2 * Z:3 * Z].reshape(block, Y, Z) - p[rows]
        v = sig[pl.ds(2 + k * block, block), R, :].reshape(block * Y, Z)
        db[rows] = slope(v).reshape(block, Y, Z)
        return carry + fold((rp * rp).reshape(block * Y, Z))

    def zadj(k, carry):
        rows = pl.ds(k * block, block)
        for a in (e3, f3):
            a[rows] = slope(a[rows].reshape(block * Y, Z)).reshape(block, Y, Z)
        return carry

    def edges():
        dedge[...] = slope(jnp.concatenate(
            [rim[f, s, 1, XI, :] for f in range(2) for s in range(2)]
            + [a[x, R, :] for a in (rho, sig) for x in (1, X + 2)], axis=0))

    def set_rows(x, carry):
        for f, a in ((0, rho), (1, sig)):
            for s in range(2):
                a[x + 2, pl.ds(7 + s * (Y + 1), 1), :] = rim[f, s, 1, pl.ds(8 + x, 1), :]
        return carry

    def set_corners():
        for f, a in ((0, rho), (1, sig)):
            for sx in range(2):
                for sy in range(2):
                    a[1 + sx * (X + 1), pl.ds(7 + sy * (Y + 1), 1), :] = (
                        rim[f, sy, 1, 7 + sx * (X + 1):8 + sx * (X + 1), :])

    XI = pl.ds(8, X)

    for k in range(ITERS):
        if k == 0:
            rims_wait(0)
            for f, a in ((0, rho), (1, sig)):
                for s in range(2):
                    rim[f, s, 0, XI, :] = yrecv[0, s, f, 1]
                    rim[f, s, 1, XI, :] = yrecv[0, s, f, 0]
                    rim[f, s, 2, XI, :] = ysend[0, s, f, 0]
                    a[pl.ds(s * (X + 2), 2), R, :] = xrecv[0, s, f]
                    for sx in range(2):
                        rim[f, s, 1, 7 + sx * (X + 1):8 + sx * (X + 1), :] = crecv[0, sx, s, f:f + 1, :]
        else:
            if k == 1:
                rims_wait(3)
            rims_wait(k)
            for s in range(2):
                for row, slot in ((0, 1), (1, 0), (2, 0)):
                    gr = (ysend[0, s, 0, 0] if row == 2 else yrecv[k, s, 0, slot])
                    gs = (ysend[0, s, 1, 0] if row == 2 else yrecv[k, s, 1, slot])
                    lo = (ysend[1, s, 0, 0] if row == 2 else yrecv[3, s, 0, slot])
                    hi = (ysend[1, s, 1, 0] if row == 2 else yrecv[3, s, 1, slot])
                    rim[0, s, row, XI, :] = jnp.minimum(jnp.maximum(rim[0, s, row, XI, :] - step_r * gr, lo), hi)
                    rim[1, s, row, XI, :] = rim[1, s, row, XI, :] - step_s * gs
                pls = pl.ds(s * (X + 2), 2)
                rho[pls, R, :] = jnp.minimum(jnp.maximum(
                    rho[pls, R, :] - step_r * xrecv[k, s, 0], xrecv[3, s, 0]), xrecv[3, s, 1])
                sig[pls, R, :] = sig[pls, R, :] - step_s * xrecv[k, s, 1]
                for sx in range(2):
                    at = slice(7 + sx * (X + 1), 8 + sx * (X + 1))
                    rim[0, s, 1, at, :] = jnp.minimum(jnp.maximum(
                        rim[0, s, 1, at, :] - step_r * crecv[k, sx, s, 0:1, :],
                        crecv[3, sx, s, 0:1, :]), crecv[3, sx, s, 1:2, :])
                    rim[1, s, 1, at, :] = rim[1, s, 1, at, :] - step_s * crecv[k, sx, s, 1:2, :]
        lax.fori_loop(0, X, set_rows, 0, unroll=4)
        set_corners()
        psq = lax.fori_loop(0, X // block, zlin, jnp.zeros((8, Z), F32))
        edges()

        for s in range(2):
            def rimstep(q, carry):
                base = pl.multiple_of(q * 8, 8)
                def vec(f):
                    a1 = rim[f, s, 1, pl.ds(9 + base, 8), :] - rim[f, s, 1, pl.ds(7 + base, 8), :]
                    a2 = rim[f, s, 2 - 2 * s, pl.ds(8 + base, 8), :] - rim[f, s, 2 * s, pl.ds(8 + base, 8), :]
                    return a1, a2, dedge[pl.ds((2 * f + s) * X + base, 8), :]
                a1, a2, a3 = vec(0)
                b1, b2, b3 = vec(1)
                c1 = a2 * b3 - a3 * b2
                c3 = a1 * b2 - a2 * b1
                rim2[s, 0, pl.ds(base, 8), :] = b3 * c1 - b1 * c3
                rim2[s, 1, pl.ds(base, 8), :] = c3 * a1 - c1 * a3
                return carry
            lax.fori_loop(0, X // 8, rimstep, 0)

        def vectors(a, x, a3):
            a1 = a[x + 1, R, :] - a[x - 1, R, :]
            a2 = a[x, pl.ds(9, Y), :] - a[x, pl.ds(7, Y), :]
            return a1, a2, a3

        def edge(x):
            at = 4 * X + (Y if x > 1 else 0)
            a1, a2, a3 = vectors(rho, x, dedge[at:at + Y, :])
            b1, b2, b3 = vectors(sig, x, dedge[at + 2 * Y:at + 3 * Y, :])
            c2 = a3 * b1 - a1 * b3
            c3 = a1 * b2 - a2 * b1
            u1[x - 1] = b2 * c3 - b3 * c2
            v1[x - 1] = c2 * a3 - c3 * a2

        edge(1)
        edge(X + 2)

        def pass1(i, acc):
            x = i + 2
            a1, a2, a3 = vectors(rho, x, da[i])
            b1, b2, b3 = vectors(sig, x, db[i])
            c1 = a2 * b3 - a3 * b2
            c2 = a3 * b1 - a1 * b3
            c3 = a1 * b2 - a2 * b1
            u1[i + 1] = b2 * c3 - b3 * c2
            v1[i + 1] = c2 * a3 - c3 * a2
            u2[i, R, :] = b3 * c1 - b1 * c3
            v2[i, R, :] = c3 * a1 - c1 * a3
            e3[i] = b1 * c2 - b2 * c1
            f3[i] = c1 * a2 - c2 * a1
            for s in range(2):
                at = pl.ds(7 + s * (Y + 1), 1)
                u2[i, at, :] = rim2[s, 0, pl.ds(i, 1), :]
                v2[i, at, :] = rim2[s, 1, pl.ds(i, 1), :]
            return acc + fold(c1 * c1 + c2 * c2 + c3 * c3)

        csq = lax.fori_loop(0, X, pass1, jnp.zeros((8, Z), F32), unroll=4)
        lax.fori_loop(0, X // block, zadj, 0)

        if k == 0:
            a, b = pw_wait(0)
            before[...] = a
            zsum[...] = b + zown
        else:
            a, b = pw_wait(k)
            before[...] = before[...] - step_s * a
            zsum[...] = zsum[...] - (step_s * xscale) * (b + wg)
        start = xscale * (float(N) - i0) * before[...] + zsum[...]

        def pass2(i, carry):
            pref, back, pg, wg, acc, nrho, nsig = carry
            v = sig[i + 2, R, :]
            pref = pref + v
            rt = xscale * pref - t[i]
            adj_s = (v1[i] - v1[i + 2]) + (v2[i, pl.ds(7, Y), :] - v2[i, pl.ds(9, Y), :]) - f3[i]
            gs = xscale * back + (BETA / 16.0) * adj_s
            back = back - rt
            adj_r = (u1[i] - u1[i + 2]) + (u2[i, pl.ds(7, Y), :] - u2[i, pl.ds(9, Y), :]) - e3[i]
            gr = (zscale * zscale) * lin[i] - gp[i] + (BETA / 16.0) * adj_r
            grho[i] = gr
            gsig[i] = gs
            acc = acc + fold(rt * rt)
            nrho = nrho + fold(gr * gr)
            nsig = nsig + fold(gs * gs)
            if k < ITERS - 1:
                gather(0, 0, i, gr)
                gather(0, 1, i, gs)
                pg = pg + gs
                wg = wg + (float(N) - i0 - i.astype(F32)) * gs
            return pref, back, pg, wg, acc, nrho, nsig

        z8 = jnp.zeros((8, Z), F32)
        _, _, pg, wg, acc, nrho, nsig = lax.fori_loop(
            0, X, pass2, (before[...], start, zero, zero, z8, z8, z8), unroll=2)
        local = (0.5 / cells) * (acc + psq + (BETA / 16.0) * csq)
        nsend[k] = jnp.concatenate([
            jnp.sum(local, axis=0, keepdims=True),
            jnp.sum(nrho, axis=0, keepdims=True),
            jnp.sum(nsig, axis=0, keepdims=True),
            jnp.zeros((5, Z), F32)], axis=0)
        nrecv[k, me] = nsend[k]
        if k < ITERS - 1:
            pwsend[0] = pg
            pwsend[1] = wg
            corners(0, 0)
            corners(0, 1)
        n_start(k)
        if k < ITERS - 1:
            rims_start(k + 1)
            pw_start(k + 1)
        tot = n_wait(k)
        obj_o[k] = tot[0, 0]
        step_r = ETA * lax.rsqrt(tot[1:2] / cells + EPSILON)
        step_s = ETA * lax.rsqrt(tot[2:3] / cells + EPSILON)

        def update(i, carry):
            rho[i + 2, R, :] = jnp.minimum(jnp.maximum(rho[i + 2, R, :] - step_r * grho[i], low[i]), high[i])
            sig[i + 2, R, :] = sig[i + 2, R, :] - step_s * gsig[i]
            return carry

        if k < ITERS - 1:
            lax.fori_loop(0, X, update, 0, unroll=4)
        else:
            def finish(i, carry):
                rho_o[i] = jnp.minimum(jnp.maximum(rho[i + 2, R, :] - step_r * grho[i], low[i]), high[i])
                sig_o[i] = sig[i + 2, R, :] - step_s * gsig[i]
                return carry

            lax.fori_loop(0, X, finish, 0, unroll=4)


def local(density, slowness, pressure_obs, time_obs, zone_map, zone_low, zone_high):
    X, Y, Z = density.shape
    nx, ny = lax.axis_size("gx"), lax.axis_size("gy")
    assert Z <= 256
    V = pltpu.VMEM
    cube = (X, Y, Z)
    padded = (X + 4, Y + 16, Z)
    dma = pltpu.SemaphoreType.DMA
    anyspace = pl.BlockSpec(memory_space=pl.ANY)
    smem = pl.BlockSpec(memory_space=pltpu.SMEM)
    scratch = [
        V(padded, F32), V(padded, F32), V(cube, F32), V(cube, F32), V(cube, F32), V(cube, F32),
        V(cube, jnp.int32), V(cube, F32), V(cube, F32), V(cube, F32), V(cube, F32),
        V((X + 2, Y, Z), F32), V((X + 2, Y, Z), F32), V((X, Y + 16, Z), F32), V((X, Y + 16, Z), F32),
        V(cube, F32), V(cube, F32), V(cube, F32), V(cube, F32), V((4 * (X + Y), Z), F32),
        V((2 * Z, 3 * Z), BF16), V((2 * Z, Z), BF16),
        V((2, 2, 3, X + 16, Z), F32), V((2, 2, X, Z), F32),
        V((2, 2, 2, 2, X, Z), F32), V((4, 2, 2, 2, X, Z), F32), V((4, 2, 2, 2, Y, Z), F32),
        V((2, 2, 2, 8, Z), F32), V((4, 2, 2, 8, Z), F32),
        V((2, Y, Z), F32), V((ITERS, nx, Y, Z), F32), V((Y, Z), F32), V((Y, Z), F32),
        V((ITERS, 8, Z), F32), V((ITERS, nx * ny, 8, Z), F32),
        dma((5,)), dma((4, 2)), dma((4, 2)), dma((4, 2, 2)), dma((4, 2, 2)),
        dma((4, 2, 2)), dma((4, 2, 2)), dma((ITERS, nx)), dma((ITERS, nx)),
        dma((nx * ny,)), dma((2, nx * ny)),
    ]
    return pl.pallas_call(
        functools.partial(kernel, nx, ny),
        out_shape=(
            pltpu.VMEM(cube, F32),
            pltpu.VMEM(cube, F32),
            jax.ShapeDtypeStruct((ITERS,), F32),
        ),
        in_specs=[smem, smem] + [anyspace] * 5,
        out_specs=(pl.BlockSpec(memory_space=pltpu.VMEM), pl.BlockSpec(memory_space=pltpu.VMEM), smem),
        scratch_shapes=scratch,
        compiler_params=pltpu.CompilerParams(
            collective_id=0, has_side_effects=True, vmem_limit_bytes=56 * 1024 * 1024),
        name="inversion",
    )(zone_low, zone_high, density, slowness, pressure_obs, time_obs, zone_map)


def solution(mesh):
    cube = P("gx", "gy", None)
    return jax.shard_map(
        local,
        mesh=mesh,
        in_specs=(cube,) * 5 + (P(), P()),
        out_specs=(cube, cube, P()),
        check_vma=False,
    )
```

profile of v0, /device:TPU:0, one launch (start us, length us, event | category | flops | bytes accessed | tf_op | source)
XLA Modules:
  0.0 56.5 jit_solution(3524317716128270830)
XLA Ops:
  0.6 53.4 %inversion.1 = (f32[64,32,128]{2,1,0:T(8,128)S(1)}, f32[64,32,128]{2,1,0:T(8,128)S(1)}, f32[3]{0:T(128)}) custom-call(f32[8]{0:T(128)} %zlow.1, f32[8]{0:T(128)} %zhigh.1, f32[64,32,128]{2,1,0:T(8,128)} %rho_h.1, f32[64,32,128]{2,1,0:T(8,128)} %sig_h.1, f32[64,32,128]{2,1,0:T(8,128)} %p_h.1, f32[64,32,128]{2,1,0:T(8,128)} %t_h.1, s32[64,32,128]{2,1,0:T(8,128)} %zone_h.1), custom_call_target="tpu_custom_call" | custom-call | tf_op jit(solution)/shard_map/inversion/pallas_call | solution.py:536
  54.1 1.0 %copy.13 = f32[64,32,128]{2,1,0:T(8,128)} copy(f32[64,32,128]{2,1,0:T(8,128)S(1)} %get-tuple-element.3) | data formatting | bytes 2097152
  55.0 0.0 copy-start
  55.0 1.0 %copy.14 = f32[64,32,128]{2,1,0:T(8,128)} copy(f32[64,32,128]{2,1,0:T(8,128)S(1)} %get-tuple-element.4) | data formatting | bytes 2097152
  56.0 0.0 copy-done
  56.0 0.5 copy.15
Async XLA Ops:
  55.0 1.0 %copy-start = (f32[3]{0:T(128)S(1)}, f32[3]{0:T(128)}, u32[]{:S(2)}) copy-start(f32[3]{0:T(128)} %get-tuple-element.11) | copy-start | bytes 40
where the time goes:
time: 56.7 us; the launch traced here: 56.5 us
  Pallas kernels  53.4 us (94%)
  local copies, waits for them, and re-layouts  2.46 us (4%)
  between operations  0.64 us (1%)
    pallas_call x1, Pallas kernels, local(): pl.pallas_call(functools.partial(kernel, nx, ny), out_shape=(pltpu.VMEM(c...  53.4 us
    unnamed x5, local copies, waits for them, and re-layouts  2.46 us

commit v1 on v0

--- a/solution.py
+++ b/solution.py
@@ -25,9 +25,9 @@
 
 def kernel(
     nx, ny,
-    zlow, zhigh, rho_h, sig_h, p_h, t_h, zone_h,
-    rho_o, sig_o, obj_o,
-    rho, sig, low, high, p, t, zone, grho, gsig, gp, lin,
+    zlow_h, zhigh_h, rho_h, sig_h, p_h, t_h, zone_h,
+    rho, sig, grho, gsig, low, high, stat,
+    zlow, zhigh, p, t, zone, gp, lin,
     u1, v1, u2, v2, e3, f3, da, db, dedge, wts, ltab,
     rim, rim2, ysend, yrecv, xrecv, csend, crecv, pwsend, pwrecv, before, zsum, nsend, nrecv,
     insem, ys, yr, xs_, xr, cs, cr, ps, pr, ns, nr,
@@ -50,6 +50,8 @@
         pltpu.make_async_copy(t_h, t, insem.at[2]),
         pltpu.make_async_copy(zone_h, zone, insem.at[3]),
         pltpu.make_async_copy(p_h, p, insem.at[4]),
+        pltpu.make_async_copy(zlow_h, zlow, insem.at[5]),
+        pltpu.make_async_copy(zhigh_h, zhigh, insem.at[6]),
     ]
     for c in loads:
         c.start()
@@ -68,6 +70,15 @@
         def _():
             for r in range(4):
                 xrecv[r, s] = jnp.zeros(xrecv.shape[2:], F32)
+
+    def other(dx, dy):
+        tx = lax.rem(mx + dx, nx) if dx else mx
+        ty = lax.rem(my + dy, ny) if dy else my
+        return tx, ty
+
+    pairs = [(dx, dy) for dx in range(nx) for dy in range(ny)][1:]
+    for dx, dy in pairs:
+        pl.semaphore_signal(barrier, inc=1, device_id=other(dx, dy), device_id_type=MESH)
 
     for s in range(2):
         zero_y(s)
@@ -80,17 +91,6 @@
                     crecv[r, sx, sy] = jnp.zeros((8, Z), F32)
     csend[...] = jnp.zeros(csend.shape, F32)
 
-    def others(d):
-        to = lax.rem(me + d, n)
-        return to, (to // ny, lax.rem(to, ny))
-
-    def greet(d, carry):
-        _, dev = others(d)
-        pl.semaphore_signal(barrier, inc=1, device_id=dev, device_id_type=MESH)
-        return carry
-
-    lax.fori_loop(1, n, greet, 0)
-
     def ycopy(r, s):
         b = 1 if r == 3 else 0
         return pltpu.make_async_remote_copy(
@@ -134,18 +134,12 @@
                 def _():
                     ccopy(r, sx, sy).start()
 
-    def rims_wait(r):
+    def yrims_wait(r):
         for s in range(2):
             @pl.when(has[s][1])
             def _():
                 ycopy(r, 1 - s).wait_recv()
                 ycopy(r, s).wait_send()
-
-            @pl.when(has[s][0])
-            def _():
-                for f in range(2):
-                    xcopy(r, 1 - s, f).wait_recv()
-                    xcopy(r, s, f).wait_send()
         for sx in range(2):
             for sy in range(2):
                 @pl.when(jnp.logical_and(has[sx][0], has[sy][1]))
@@ -153,6 +147,14 @@
                     ccopy(r, 1 - sx, 1 - sy).wait_recv()
                     ccopy(r, sx, sy).wait_send()
 
+    def xrims_wait(r):
+        for s in range(2):
+            @pl.when(has[s][0])
+            def _():
+                for f in range(2):
+                    xcopy(r, 1 - s, f).wait_recv()
+                    xcopy(r, s, f).wait_send()
+
     def pwcopy(r, tx, slot):
         later = jnp.where(tx > mx, 0, 1)
         return pltpu.make_async_remote_copy(
@@ -161,10 +163,8 @@
             device_id=(tx, my), device_id_type=MESH)
 
     def pw_start(r):
-        def go(d, carry):
-            pwcopy(r, lax.rem(mx + d, nx), mx).start()
-            return carry
-        lax.fori_loop(1, nx, go, 0)
+        for dx in range(1, nx):
+            pwcopy(r, other(dx, 0)[0], mx).start()
 
     def pw_wait(r):
         def go(d, carry):
@@ -183,30 +183,21 @@
         zero = jnp.zeros((Y, Z), F32)
         return lax.fori_loop(1, nx, add, (zero, zero))
 
-    def ncopy(r, to, dev, slot):
-        return pltpu.make_async_remote_copy(
-            src_ref=nsend.at[r], dst_ref=nrecv.at[r, slot],
-            send_sem=ns.at[to], recv_sem=nr.at[r % 2, slot],
-            device_id=dev, device_id_type=MESH)
-
     def n_start(r):
-        def go(d, carry):
-            to, dev = others(d)
-            ncopy(r, to, dev, me).start()
-            return carry
-        lax.fori_loop(1, n, go, 0)
+        for d, (dx, dy) in enumerate(pairs):
+            pltpu.make_async_remote_copy(
+                src_ref=nsend.at[r, pl.ds(0, 1)], dst_ref=nrecv.at[r, pl.ds(d, 1)],
+                send_sem=ns.at[r], recv_sem=nr.at[r],
+                device_id=other(dx, dy), device_id_type=MESH).start()
 
     def n_wait(r):
-        def go(d, carry):
-            to, dev = others(d)
-            ncopy(r, to, dev, to).wait_recv()
-            ncopy(r, to, dev, to).wait_send()
-            return carry
-        lax.fori_loop(1, n, go, 0)
-        tot = nrecv[r, 0]
-        for s in range(1, n):
-            tot = tot + nrecv[r, s]
-        return jnp.sum(tot, axis=1, keepdims=True)
+        rows = nrecv.at[r, pl.ds(0, n - 1)]
+        every = pltpu.make_async_remote_copy(
+            src_ref=rows, dst_ref=rows, send_sem=ns.at[r], recv_sem=nr.at[r],
+            device_id=other(0, 1), device_id_type=MESH)
+        every.wait_recv()
+        every.wait_send()
+        return jnp.sum(nrecv[r], axis=0, keepdims=True)
 
     def fold(v):
         out = v[0:8]
@@ -228,8 +219,9 @@
 
     zero = jnp.zeros((Y, Z), F32)
 
-    loads[0].wait()
-    loads[2].wait()
+    with jax.named_scope("load02"):
+        loads[0].wait()
+        loads[2].wait()
 
     def sums(x, carry):
         a, b, c = carry
@@ -251,11 +243,13 @@
     lax.fori_loop(0, X, copy_rho, 0, unroll=4)
     corners(0, 0)
     corners(0, 1)
-    pl.semaphore_wait(barrier, n - 1)
+    with jax.named_scope("barrier"):
+        pl.semaphore_wait(barrier, n - 1)
     rims_start(0)
     pw_start(0)
 
-    loads[3].wait()
+    for c in loads[3:]:
+        c.wait()
 
     def bounds(x, carry):
         ids = zone[x]
@@ -274,7 +268,6 @@
     lax.fori_loop(0, X, bounds, 0, unroll=2)
     corners(1, 0)
     corners(1, 1)
-    rims_start(3)
 
     ri = lax.broadcasted_iota(jnp.int32, (Z, Z), 0)
     ci = lax.broadcasted_iota(jnp.int32, (Z, Z), 1)
@@ -295,7 +288,6 @@
     def slope(v):
         return jnp.dot(split(v), band2[...], preferred_element_type=F32)
 
-    loads[4].wait()
 
     def pback(k, carry):
         rows = pl.ds(k * block, block)
@@ -325,8 +317,11 @@
 
     def edges():
         dedge[...] = slope(jnp.concatenate(
-            [rim[f, s, 1, XI, :] for f in range(2) for s in range(2)]
-            + [a[x, R, :] for a in (rho, sig) for x in (1, X + 2)], axis=0))
+            [rim[f, s, 1, XI, :] for f in range(2) for s in range(2)], axis=0))
+
+    def xedges():
+        return slope(jnp.concatenate(
+            [a[x, R, :] for a in (rho, sig) for x in (1, X + 2)], axis=0))
 
     def set_rows(x, carry):
         for f, a in ((0, rho), (1, sig)):
@@ -345,19 +340,22 @@
 
     for k in range(ITERS):
         if k == 0:
-            rims_wait(0)
+            with jax.named_scope("zlin"):
+                psq = lax.fori_loop(0, X // block, zlin, jnp.zeros((8, Z), F32))
+            with jax.named_scope("yrimwait"):
+                yrims_wait(0)
             for f, a in ((0, rho), (1, sig)):
                 for s in range(2):
                     rim[f, s, 0, XI, :] = yrecv[0, s, f, 1]
                     rim[f, s, 1, XI, :] = yrecv[0, s, f, 0]
                     rim[f, s, 2, XI, :] = ysend[0, s, f, 0]
-                    a[pl.ds(s * (X + 2), 2), R, :] = xrecv[0, s, f]
                     for sx in range(2):
                         rim[f, s, 1, 7 + sx * (X + 1):8 + sx * (X + 1), :] = crecv[0, sx, s, f:f + 1, :]
         else:
-            if k == 1:
-                rims_wait(3)
-            rims_wait(k)
+            with jax.named_scope("yrimwait"):
+                if k == 1:
+                    yrims_wait(3)
+                yrims_wait(k)
             for s in range(2):
                 for row, slot in ((0, 1), (1, 0), (2, 0)):
                     gr = (ysend[0, s, 0, 0] if row == 2 else yrecv[k, s, 0, slot])
@@ -366,20 +364,20 @@
                     hi = (ysend[1, s, 1, 0] if row == 2 else yrecv[3, s, 1, slot])
                     rim[0, s, row, XI, :] = jnp.minimum(jnp.maximum(rim[0, s, row, XI, :] - step_r * gr, lo), hi)
                     rim[1, s, row, XI, :] = rim[1, s, row, XI, :] - step_s * gs
-                pls = pl.ds(s * (X + 2), 2)
-                rho[pls, R, :] = jnp.minimum(jnp.maximum(
-                    rho[pls, R, :] - step_r * xrecv[k, s, 0], xrecv[3, s, 0]), xrecv[3, s, 1])
-                sig[pls, R, :] = sig[pls, R, :] - step_s * xrecv[k, s, 1]
                 for sx in range(2):
                     at = slice(7 + sx * (X + 1), 8 + sx * (X + 1))
                     rim[0, s, 1, at, :] = jnp.minimum(jnp.maximum(
                         rim[0, s, 1, at, :] - step_r * crecv[k, sx, s, 0:1, :],
                         crecv[3, sx, s, 0:1, :]), crecv[3, sx, s, 1:2, :])
                     rim[1, s, 1, at, :] = rim[1, s, 1, at, :] - step_s * crecv[k, sx, s, 1:2, :]
-        lax.fori_loop(0, X, set_rows, 0, unroll=4)
-        set_corners()
-        psq = lax.fori_loop(0, X // block, zlin, jnp.zeros((8, Z), F32))
-        edges()
+        with jax.named_scope("setrows"):
+            lax.fori_loop(0, X, set_rows, 0, unroll=4)
+            set_corners()
+        if k > 0:
+            with jax.named_scope("zlin"):
+                psq = lax.fori_loop(0, X // block, zlin, jnp.zeros((8, Z), F32))
+        with jax.named_scope("edges"):
+            edges()
 
         for s in range(2):
             def rimstep(q, carry):
@@ -395,24 +393,22 @@
                 rim2[s, 0, pl.ds(base, 8), :] = b3 * c1 - b1 * c3
                 rim2[s, 1, pl.ds(base, 8), :] = c3 * a1 - c1 * a3
                 return carry
-            lax.fori_loop(0, X // 8, rimstep, 0)
+            with jax.named_scope("rimstep"):
+                lax.fori_loop(0, X // 8, rimstep, 0)
 
         def vectors(a, x, a3):
             a1 = a[x + 1, R, :] - a[x - 1, R, :]
             a2 = a[x, pl.ds(9, Y), :] - a[x, pl.ds(7, Y), :]
             return a1, a2, a3
 
-        def edge(x):
-            at = 4 * X + (Y if x > 1 else 0)
-            a1, a2, a3 = vectors(rho, x, dedge[at:at + Y, :])
-            b1, b2, b3 = vectors(sig, x, dedge[at + 2 * Y:at + 3 * Y, :])
+        def edge(x, ds):
+            at = Y if x > 1 else 0
+            a1, a2, a3 = vectors(rho, x, ds[at:at + Y])
+            b1, b2, b3 = vectors(sig, x, ds[at + 2 * Y:at + 3 * Y])
             c2 = a3 * b1 - a1 * b3
             c3 = a1 * b2 - a2 * b1
             u1[x - 1] = b2 * c3 - b3 * c2
             v1[x - 1] = c2 * a3 - c3 * a2
-
-        edge(1)
-        edge(X + 2)
 
         def pass1(i, acc):
             x = i + 2
@@ -433,15 +429,43 @@
                 v2[i, at, :] = rim2[s, 1, pl.ds(i, 1), :]
             return acc + fold(c1 * c1 + c2 * c2 + c3 * c3)
 
-        csq = lax.fori_loop(0, X, pass1, jnp.zeros((8, Z), F32), unroll=4)
-        lax.fori_loop(0, X // block, zadj, 0)
-
+        with jax.named_scope("pass1"):
+            csq = lax.fori_loop(2, X - 2, pass1, jnp.zeros((8, Z), F32), unroll=4)
+            csq = pass1(1, csq)
+            csq = pass1(X - 2, csq)
+        with jax.named_scope("xrimwait"):
+            if k == 1:
+                xrims_wait(3)
+            xrims_wait(k)
+        for s in range(2):
+            pls = pl.ds(s * (X + 2), 2)
+            if k == 0:
+                rho[pls, R, :] = xrecv[0, s, 0]
+                sig[pls, R, :] = xrecv[0, s, 1]
+            else:
+                rho[pls, R, :] = jnp.minimum(jnp.maximum(
+                    rho[pls, R, :] - step_r * xrecv[k, s, 0], xrecv[3, s, 0]), xrecv[3, s, 1])
+                sig[pls, R, :] = sig[pls, R, :] - step_s * xrecv[k, s, 1]
         if k == 0:
-            a, b = pw_wait(0)
+            with jax.named_scope("rims3start"):
+                rims_start(3)
+        with jax.named_scope("edge"):
+            ds = xedges()
+            edge(1, ds)
+            edge(X + 2, ds)
+            csq = pass1(0, csq)
+            csq = pass1(X - 1, csq)
+        with jax.named_scope("zadj"):
+            lax.fori_loop(0, X // block, zadj, 0)
+
+        if k == 0:
+            with jax.named_scope("pwwait"):
+                a, b = pw_wait(0)
             before[...] = a
             zsum[...] = b + zown
         else:
-            a, b = pw_wait(k)
+            with jax.named_scope("pwwait"):
+                a, b = pw_wait(k)
             before[...] = before[...] - step_s * a
             zsum[...] = zsum[...] - (step_s * xscale) * (b + wg)
         start = xscale * (float(N) - i0) * before[...] + zsum[...]
@@ -469,28 +493,35 @@
             return pref, back, pg, wg, acc, nrho, nsig
 
         z8 = jnp.zeros((8, Z), F32)
-        _, _, pg, wg, acc, nrho, nsig = lax.fori_loop(
-            0, X, pass2, (before[...], start, zero, zero, z8, z8, z8), unroll=2)
+        with jax.named_scope("pass2"):
+            _, _, pg, wg, acc, nrho, nsig = lax.fori_loop(
+                0, X, pass2, (before[...], start, zero, zero, z8, z8, z8), unroll=2)
         local = (0.5 / cells) * (acc + psq + (BETA / 16.0) * csq)
-        nsend[k] = jnp.concatenate([
-            jnp.sum(local, axis=0, keepdims=True),
-            jnp.sum(nrho, axis=0, keepdims=True),
-            jnp.sum(nsig, axis=0, keepdims=True),
-            jnp.zeros((5, Z), F32)], axis=0)
-        nrecv[k, me] = nsend[k]
+        lane = lax.broadcasted_iota(jnp.int32, (1, Z), 1)
+
+        def total(v):
+            return jnp.sum(jnp.sum(v, axis=0, keepdims=True), axis=1, keepdims=True)
+
+        row = jnp.where(lane < 1, total(nrho), jnp.where(lane < 2, total(nsig), total(local)))
+        nsend[k, 0:1] = row
+        nrecv[k, n - 1:n] = row
+        with jax.named_scope("nstart"):
+            n_start(k)
         if k < ITERS - 1:
             pwsend[0] = pg
             pwsend[1] = wg
             corners(0, 0)
             corners(0, 1)
-        n_start(k)
         if k < ITERS - 1:
-            rims_start(k + 1)
-            pw_start(k + 1)
-        tot = n_wait(k)
-        obj_o[k] = tot[0, 0]
-        step_r = ETA * lax.rsqrt(tot[1:2] / cells + EPSILON)
-        step_s = ETA * lax.rsqrt(tot[2:3] / cells + EPSILON)
+            with jax.named_scope("rimstart"):
+                rims_start(k + 1)
+                pw_start(k + 1)
+        with jax.named_scope("nwait"):
+            tot = n_wait(k)
+        steps = ETA * lax.rsqrt(tot / cells + EPSILON)
+        step_r = jnp.broadcast_to(steps[0:1, 0:1], (1, Z))
+        step_s = jnp.broadcast_to(steps[0:1, 1:2], (1, Z))
+        stat[k:k + 1, :] = jnp.broadcast_to(tot[0:1, 2:3], (1, Z))
 
         def update(i, carry):
             rho[i + 2, R, :] = jnp.minimum(jnp.maximum(rho[i + 2, R, :] - step_r * grho[i], low[i]), high[i])
@@ -498,14 +529,38 @@
             return carry
 
         if k < ITERS - 1:
-            lax.fori_loop(0, X, update, 0, unroll=4)
+            with jax.named_scope("update"):
+                lax.fori_loop(0, X, update, 0, unroll=4)
         else:
-            def finish(i, carry):
-                rho_o[i] = jnp.minimum(jnp.maximum(rho[i + 2, R, :] - step_r * grho[i], low[i]), high[i])
-                sig_o[i] = sig[i + 2, R, :] - step_s * gsig[i]
-                return carry
-
-            lax.fori_loop(0, X, finish, 0, unroll=4)
+            stat[ITERS:ITERS + 1, :] = step_r
+            stat[ITERS + 1:ITERS + 2, :] = step_s
+
+
+def finish(rho, sig, grho, gsig, low, high, stat, rho_o, sig_o, obj_o, rho_b, sig_b, obj, sems):
+    X, Y, Z = grho.shape
+    R = pl.ds(8, Y)
+    seen = stat[...]
+    for k in range(ITERS):
+        obj[k] = seen[k, 0]
+    copies = [pltpu.make_async_copy(obj, obj_o, sems.at[0])]
+    copies[0].start()
+    step_r = stat[ITERS:ITERS + 1, :]
+    step_s = stat[ITERS + 1:ITERS + 2, :]
+
+    def move(i, carry):
+        rho_b[i] = jnp.minimum(jnp.maximum(rho[i + 2, R, :] - step_r * grho[i], low[i]), high[i])
+        sig_b[i] = sig[i + 2, R, :] - step_s * gsig[i]
+        return carry
+
+    parts = 4
+    for c in range(parts):
+        lax.fori_loop(c * X // parts, (c + 1) * X // parts, move, 0, unroll=4)
+        rows = pl.ds(c * X // parts, X // parts)
+        for f, (a, b) in enumerate(((rho_b, rho_o), (sig_b, sig_o))):
+            copies.append(pltpu.make_async_copy(a.at[rows], b.at[rows], sems.at[1 + 2 * c + f]))
+            copies[-1].start()
+    for c in copies:
+        c.wait()
 
 
 def local(density, slowness, pressure_obs, time_obs, zone_map, zone_low, zone_high):
@@ -517,36 +572,48 @@
     padded = (X + 4, Y + 16, Z)
     dma = pltpu.SemaphoreType.DMA
     anyspace = pl.BlockSpec(memory_space=pl.ANY)
-    smem = pl.BlockSpec(memory_space=pltpu.SMEM)
+    zones = zone_low.shape[0]
     scratch = [
-        V(padded, F32), V(padded, F32), V(cube, F32), V(cube, F32), V(cube, F32), V(cube, F32),
-        V(cube, jnp.int32), V(cube, F32), V(cube, F32), V(cube, F32), V(cube, F32),
+        pltpu.SMEM((zones,), F32), pltpu.SMEM((zones,), F32),
+        V(cube, F32), V(cube, F32),
+        V(cube, jnp.int32), V(cube, F32), V(cube, F32),
         V((X + 2, Y, Z), F32), V((X + 2, Y, Z), F32), V((X, Y + 16, Z), F32), V((X, Y + 16, Z), F32),
-        V(cube, F32), V(cube, F32), V(cube, F32), V(cube, F32), V((4 * (X + Y), Z), F32),
+        V(cube, F32), V(cube, F32), V(cube, F32), V(cube, F32), V((4 * X, Z), F32),
         V((2 * Z, 3 * Z), BF16), V((2 * Z, Z), BF16),
         V((2, 2, 3, X + 16, Z), F32), V((2, 2, X, Z), F32),
         V((2, 2, 2, 2, X, Z), F32), V((4, 2, 2, 2, X, Z), F32), V((4, 2, 2, 2, Y, Z), F32),
         V((2, 2, 2, 8, Z), F32), V((4, 2, 2, 8, Z), F32),
         V((2, Y, Z), F32), V((ITERS, nx, Y, Z), F32), V((Y, Z), F32), V((Y, Z), F32),
-        V((ITERS, 8, Z), F32), V((ITERS, nx * ny, 8, Z), F32),
-        dma((5,)), dma((4, 2)), dma((4, 2)), dma((4, 2, 2)), dma((4, 2, 2)),
+        V((ITERS, 8, Z), F32), V((ITERS, nx * ny, Z), F32),
+        dma((7,)), dma((4, 2)), dma((4, 2)), dma((4, 2, 2)), dma((4, 2, 2)),
         dma((4, 2, 2)), dma((4, 2, 2)), dma((ITERS, nx)), dma((ITERS, nx)),
-        dma((nx * ny,)), dma((2, nx * ny)),
+        dma((ITERS,)), dma((ITERS,)),
     ]
+    inside = pl.BlockSpec(memory_space=pltpu.VMEM)
+    state = pl.pallas_call(
+        functools.partial(kernel, nx, ny),
+        out_shape=(pltpu.VMEM(padded, F32), pltpu.VMEM(padded, F32))
+        + (pltpu.VMEM(cube, F32),) * 4 + (pltpu.VMEM((8, Z), F32),),
+        in_specs=[pl.BlockSpec(memory_space=pltpu.HBM)] * 7,
+        out_specs=(inside,) * 7,
+        scratch_shapes=scratch,
+        compiler_params=pltpu.CompilerParams(
+            collective_id=0, has_side_effects=True, vmem_limit_bytes=48 * 1024 * 1024),
+        name="inversion",
+    )(zone_low, zone_high, density, slowness, pressure_obs, time_obs, zone_map)
     return pl.pallas_call(
-        functools.partial(kernel, nx, ny),
+        finish,
         out_shape=(
-            pltpu.VMEM(cube, F32),
-            pltpu.VMEM(cube, F32),
+            jax.ShapeDtypeStruct(cube, F32),
+            jax.ShapeDtypeStruct(cube, F32),
             jax.ShapeDtypeStruct((ITERS,), F32),
         ),
-        in_specs=[smem, smem] + [anyspace] * 5,
-        out_specs=(pl.BlockSpec(memory_space=pltpu.VMEM), pl.BlockSpec(memory_space=pltpu.VMEM), smem),
-        scratch_shapes=scratch,
-        compiler_params=pltpu.CompilerParams(
-            collective_id=0, has_side_effects=True, vmem_limit_bytes=56 * 1024 * 1024),
-        name="inversion",
-    )(zone_low, zone_high, density, slowness, pressure_obs, time_obs, zone_map)
+        in_specs=[inside] * 7,
+        out_specs=(anyspace,) * 3,
+        scratch_shapes=[V(cube, F32), V(cube, F32), pltpu.SMEM((ITERS,), F32), dma((9,))],
+        compiler_params=pltpu.CompilerParams(vmem_limit_bytes=20 * 1024 * 1024),
+        name="finish",
+    )(*(pltpu.with_memory_space_constraint(a, pltpu.VMEM) for a in state))
 
 
 def solution(mesh):

time: 56.7 us -> 47.5 us (0.84)
  Pallas kernels: 53.4 us -> 46.7 us
  local copies, waits for them, and re-layouts: 2.46 us -> 0 us
    pallas_call x1 -> x2, Pallas kernels: 53.4 us -> 46.7 us  [the longest x1 45.2 us: local(): pl.pallas_call(functools.partial(kernel, nx, ny), out_shape=(pltpu.VMEM(p...]
    unnamed x5 -> x0, local copies, waits for them, and re-layouts: 2.46 us -> none
where the time goes in v1:
time: 47.5 us; the launch traced here: 47.4 us
  Pallas kernels  46.7 us (98%)
  between operations  0.64 us (1%)
    pallas_call x1, Pallas kernels, local(): pl.pallas_call(functools.partial(kernel, nx, ny), out_shape=(pltpu.VMEM(p...  45.2 us
    pallas_call x1, Pallas kernels, local(): pl.pallas_call(finish, out_shape=(jax.ShapeDtypeStruct(cube, F32), jax.Sh...  1.51 us

profile of v1, /device:TPU:0, one launch (start us, length us, event | category | flops | bytes accessed | tf_op | source)
XLA Modules:
  0.0 47.4 jit_solution(5104371875931468881)
XLA Ops:
  0.6 45.2 %inversion.1 = (f32[68,48,128]{2,1,0:T(8,128)S(1)}, f32[68,48,128]{2,1,0:T(8,128)S(1)}, f32[64,32,128]{2,1,0:T(8,128)S(1)}, f32[64,32,128]{2,1,0:T(8,128)S(1)}, ...) custom-call(f32[8]{0:T(128)} %zlow_h.1, f32[8]{0:T(128)} %zhigh_h.1, ...), custom_call_target="tpu_custom_call" | custom-call | tf_op jit(solution)/shard_map/inversion/pallas_call | solution.py:593
  45.9 1.5 %finish.1 = (f32[64,32,128]{2,1,0:T(8,128)}, f32[64,32,128]{2,1,0:T(8,128)}, f32[3]{0:T(128)}) custom-call(f32[68,48,128]{2,1,0:T(8,128)S(1)} %get-tuple-element.10.rho, f32[68,48,128]{2,1,0:T(8,128)S(1)} %get-tuple-element.11.sig, f32[64,32,128]{2,1,0:T(8,128)S(1)} %get-tuple-element.12.grho, f32[64,32,128]{2,1,0:T(8,128)S(1)} %get-tuple-element.13.gsig, ...), custom_call_target="tpu_custom_call" | custom-call | tf_op jit(solution)/shard_map/finish/pallas_call | solution.py:604

commit v2 on v1

v2 whole, which is shorter than its diff:
```python
import functools
import math

import jax
import jax.numpy as jnp
from jax import lax
from jax.experimental import pallas as pl
from jax.experimental.pallas import tpu as pltpu
from jax.sharding import PartitionSpec as P

ITERS = 3
BETA = 1.0
ETA = 0.5
EPSILON = 1e-06
MESH = pl.DeviceIdType.MESH
F32 = jnp.float32
BF16 = jnp.bfloat16
BOUNDS = 3
BANK = (0, 1, 0, 2)
UNROLL2 = 2
scope = jax.named_scope


def split(v):
    hi = v.astype(BF16)
    lo = (v - hi.astype(F32)).astype(BF16)
    return jnp.concatenate([hi, lo], axis=-1)


def kernel(
    nx, ny,
    zlow_h, zhigh_h, rho_h, sig_h, p_h, t_h, zone_h,
    both, grad, lim, stat,
    zlow, zhigh, p, t, zone, gp, lin,
    u1, v1, u2, v2, e3, f3, da, db, dedge, wts, ltab,
    rim, rim2, ysend, yrecv, xrecv, csend, crecv, pwsend, pwrecv, before, zsum, nsend, nrecv,
    insem, ys, yr, xs_, xr, cs, cr, ps, pr, ns, nr,
):
    X, Y, Z = p.shape
    rho, sig = both.at[0], both.at[1]
    grho, gsig = grad.at[0], grad.at[1]
    low, high = lim.at[0], lim.at[1]
    mx, my = lax.axis_index("gx"), lax.axis_index("gy")
    n = nx * ny
    N = nx * X
    cells = float(N * ny * Y * Z)
    zscale = 1.0 / math.sqrt(Z)
    xscale = 1.0 / math.sqrt(N)
    R = pl.ds(8, Y)
    XI = pl.ds(8, X)
    i0 = (mx * X).astype(F32)

    inner = (pl.ds(2, X), R)
    loads = [
        pltpu.make_async_copy(sig_h, sig.at[inner], insem.at[0]),
        pltpu.make_async_copy(rho_h, rho.at[inner], insem.at[1]),
        pltpu.make_async_copy(t_h, t, insem.at[2]),
        pltpu.make_async_copy(zone_h, zone, insem.at[3]),
        pltpu.make_async_copy(p_h, p, insem.at[4]),
        pltpu.make_async_copy(zlow_h, zlow, insem.at[5]),
        pltpu.make_async_copy(zhigh_h, zhigh, insem.at[6]),
    ]
    for c in loads:
        c.start()
    barrier = pltpu.get_barrier_semaphore()

    has = {0: (mx > 0, my > 0), 1: (mx < nx - 1, my < ny - 1)}
    sides = [(sx, sy) for sx in range(2) for sy in range(2)]

    def other(dx, dy):
        tx = lax.rem(mx + dx, nx) if dx else mx
        ty = lax.rem(my + dy, ny) if dy else my
        return tx, ty

    pairs = [(dx, dy) for dx in range(nx) for dy in range(ny)][1:]
    for dx, dy in pairs:
        pl.semaphore_signal(barrier, inc=1, device_id=other(dx, dy), device_id_type=MESH)

    for s in range(2):
        @pl.when(jnp.logical_not(has[s][1]))
        def _():
            for r in range(4):
                yrecv[r, s] = jnp.zeros(yrecv.shape[2:], F32)

        @pl.when(jnp.logical_not(has[s][0]))
        def _():
            for r in range(4):
                xrecv[r, s] = jnp.zeros(xrecv.shape[2:], F32)
    for sx, sy in sides:
        @pl.when(jnp.logical_not(jnp.logical_and(has[sx][0], has[sy][1])))
        def _():
            for r in range(4):
                crecv[r, sx, sy] = jnp.zeros((8, Z), F32)

    def ycopy(r, s):
        b = 1 if r == BOUNDS else 0
        return pltpu.make_async_remote_copy(
            src_ref=ysend.at[b, s], dst_ref=yrecv.at[r, 1 - s],
            send_sem=ys.at[s], recv_sem=yr.at[BANK[r], 1 - s],
            device_id=(mx, my + (2 * s - 1)), device_id_type=MESH)

    def xcopy(r, s):
        if r == 0:
            src = both.at[:, pl.ds(2 + s * (X - 2), 2), R]
        else:
            src = (lim if r == BOUNDS else grad).at[:, pl.ds(s * (X - 2), 2)]
        return pltpu.make_async_remote_copy(
            src_ref=src, dst_ref=xrecv.at[r, 1 - s],
            send_sem=xs_.at[s], recv_sem=xr.at[BANK[r], 1 - s],
            device_id=(mx + (2 * s - 1), my), device_id_type=MESH)

    def ccopy(r, sx, sy):
        b = 1 if r == BOUNDS else 0
        return pltpu.make_async_remote_copy(
            src_ref=csend.at[b, sx, sy, pl.ds(0, 2)], dst_ref=crecv.at[r, 1 - sx, 1 - sy, pl.ds(0, 2)],
            send_sem=cs.at[sx, sy], recv_sem=cr.at[BANK[r], 1 - sx, 1 - sy],
            device_id=(mx + (2 * sx - 1), my + (2 * sy - 1)), device_id_type=MESH)

    def rims_start(r):
        for sx, sy in sides:
            @pl.when(jnp.logical_and(has[sx][0], has[sy][1]))
            def _():
                ccopy(r, sx, sy).start()
        for s in range(2):
            @pl.when(has[s][1])
            def _():
                ycopy(r, s).start()

            @pl.when(has[s][0])
            def _():
                xcopy(r, s).start()

    def yrims_wait(r):
        for s in range(2):
            @pl.when(has[s][1])
            def _():
                ycopy(r, 1 - s).wait_recv()
        for sx, sy in sides:
            @pl.when(jnp.logical_and(has[sx][0], has[sy][1]))
            def _():
                ccopy(r, 1 - sx, 1 - sy).wait_recv()

    def xrims_wait(r):
        for s in range(2):
            @pl.when(has[s][0])
            def _():
                xcopy(r, 1 - s).wait_recv()

    def rims_sent(r):
        for s in range(2):
            @pl.when(has[s][1])
            def _():
                ycopy(r, s).wait_send()

            @pl.when(has[s][0])
            def _():
                xcopy(r, s).wait_send()
        for sx, sy in sides:
            @pl.when(jnp.logical_and(has[sx][0], has[sy][1]))
            def _():
                ccopy(r, sx, sy).wait_send()

    def pw_start(r):
        for dx in range(1, nx):
            tx, _ = other(dx, 0)
            pltpu.make_async_remote_copy(
                src_ref=pwsend.at[jnp.where(tx > mx, 0, 1)], dst_ref=pwrecv.at[r, dx - 1],
                send_sem=ps.at[0], recv_sem=pr.at[r % 2],
                device_id=(tx, my), device_id_type=MESH).start()

    def pw_wait(r):
        slots = pwrecv.at[r, pl.ds(0, nx - 1)]
        every = pltpu.make_async_remote_copy(
            src_ref=slots, dst_ref=slots, send_sem=ps.at[0], recv_sem=pr.at[r % 2],
            device_id=other(1, 0), device_id_type=MESH)
        every.wait_recv()
        every.wait_send()
        a = jnp.zeros((Y, Z), F32)
        b = jnp.zeros((Y, Z), F32)
        for dx in range(1, nx):
            w = jnp.where(dx <= mx, 1.0, 0.0)
            v = pwrecv[r, dx - 1]
            a = a + v * w
            b = b + v * (1.0 - w)
        return a, b

    def n_start(r):
        for d, (dx, dy) in enumerate(pairs):
            pltpu.make_async_remote_copy(
                src_ref=nsend.at[r, pl.ds(0, 1)], dst_ref=nrecv.at[r, pl.ds(d, 1)],
                send_sem=ns.at[0], recv_sem=nr.at[r % 2],
                device_id=other(dx, dy), device_id_type=MESH).start()

    def n_wait(r):
        rows = nrecv.at[r, pl.ds(0, n - 1)]
        every = pltpu.make_async_remote_copy(
            src_ref=rows, dst_ref=rows, send_sem=ns.at[0], recv_sem=nr.at[r % 2],
            device_id=other(0, 1), device_id_type=MESH)
        every.wait_recv()
        every.wait_send()
        return jnp.sum(nrecv[r], axis=0, keepdims=True)

    def fold(v):
        out = v[0:8]
        for k in range(8, v.shape[0], 8):
            out = out + v[k:k + 8]
        return out

    def gather(b, f, x, v):
        row = pl.ds(x, 1)
        ysend[b, 0, f, 0, row, :] = v[0:1]
        ysend[b, 0, f, 1, row, :] = v[1:2]
        ysend[b, 1, f, 0, row, :] = v[Y - 1:Y]
        ysend[b, 1, f, 1, row, :] = v[Y - 2:Y - 1]

    def corners(b):
        for f in range(2):
            for sx, sy in sides:
                csend[b, sx, sy, f:f + 1, :] = ysend[b, sy, f, 0, sx * (X - 1):sx * (X - 1) + 1, :]

    def slope(v):
        lane = lax.broadcasted_iota(jnp.int32, v.shape, 1)
        up = jnp.where(lane < Z - 1, pltpu.roll(v, Z - 1, 1), 0.0)
        return up - jnp.where(lane > 0, pltpu.roll(v, 1, 1), 0.0)

    zero = jnp.zeros((Y, Z), F32)
    z8 = jnp.zeros((8, Z), F32)

    with scope("load02"):
        loads[0].wait()
        loads[2].wait()

    def sums(x, carry):
        a, b, c = carry
        v = sig[x + 2, R, :]
        gather(0, 1, x, v)
        weight = float(N) - i0 - x.astype(F32)
        return a + v, b + weight * v, c + t[x]

    psum_, wsum, tsum = lax.fori_loop(0, X, sums, (zero, zero, zero), unroll=4)
    zown = xscale * wsum - tsum
    pwsend[0] = psum_
    pwsend[1] = zown
    loads[1].wait()

    def copy_rho(x, carry):
        gather(0, 0, x, rho[x + 2, R, :])
        return carry

    lax.fori_loop(0, X, copy_rho, 0, unroll=4)
    corners(0)
    with scope("barrier"):
        pl.semaphore_wait(barrier, n - 1)
    with scope("rims0start"):
        rims_start(0)
        pw_start(0)

    for c in loads[3:]:
        c.wait()

    def bounds(x, carry):
        ids = zone[x]
        lo = jnp.zeros((Y, Z), F32)
        hi = jnp.zeros((Y, Z), F32)
        for k in range(zlow.shape[0]):
            hit = ids == k
            lo = jnp.where(hit, zlow[k], lo)
            hi = jnp.where(hit, zhigh[k], hi)
        low[x] = lo
        high[x] = hi
        gather(1, 0, x, lo)
        gather(1, 1, x, hi)
        return carry

    with scope("bounds"):
        lax.fori_loop(0, X, bounds, 0, unroll=2)
        corners(1)

    ri = lax.broadcasted_iota(jnp.int32, (Z, Z), 0)
    ci = lax.broadcasted_iota(jnp.int32, (Z, Z), 1)
    m = (Z - jnp.maximum(ri, ci)).astype(F32).astype(BF16)
    u = jnp.where(ri <= ci, 1.0, 0.0).astype(BF16)
    band = jnp.where(ri == ci + 1, 1.0, jnp.where(ri == ci - 1, -1.0, 0.0)).astype(BF16)
    l = jnp.where(ri >= ci, 1.0, 0.0).astype(BF16)
    for half in (slice(0, Z), slice(Z, 2 * Z)):
        wts[half, 0:Z] = m
        wts[half, Z:2 * Z] = band
        wts[half, 2 * Z:3 * Z] = u
        ltab[half] = l

    with scope("pback"):
        v = p[...].reshape(X * Y, Z)
        out = jnp.dot(split(v), ltab[...], preferred_element_type=F32)
        gp[...] = (out * zscale).reshape(X, Y, Z)

    def zslope(v):
        return jnp.dot(split(v), wts[:, Z:2 * Z], preferred_element_type=F32)

    def zlin():
        v = rho[inner[0], R, :].reshape(X * Y, Z)
        out = jnp.dot(split(v), wts[...], preferred_element_type=F32)
        lin[...] = out[:, 0:Z].reshape(X, Y, Z)
        da[...] = out[:, Z:2 * Z].reshape(X, Y, Z)
        rp = zscale * out[:, 2 * Z:3 * Z].reshape(X, Y, Z) - p[...]
        v = sig[inner[0], R, :].reshape(X * Y, Z)
        db[...] = zslope(v).reshape(X, Y, Z)
        return fold((rp * rp).reshape(X * Y, Z))

    def edges():
        dedge[...] = slope(jnp.concatenate(
            [rim[f, s, 1, XI, :] for f in range(2) for s in range(2)], axis=0))

    def set_rows(x, carry):
        for f, a in ((0, rho), (1, sig)):
            for s in range(2):
                a[x + 2, pl.ds(7 + s * (Y + 1), 1), :] = rim[f, s, 1, pl.ds(8 + x, 1), :]
        return carry

    def set_corners():
        for f, a in ((0, rho), (1, sig)):
            for sx, sy in sides:
                a[1 + sx * (X + 1), pl.ds(7 + sy * (Y + 1), 1), :] = (
                    rim[f, sy, 1, 7 + sx * (X + 1):8 + sx * (X + 1), :])

    for k in range(ITERS):
        if k > 0:
            def update(i, carry):
                rho[i + 2, R, :] = jnp.minimum(jnp.maximum(rho[i + 2, R, :] - step_r * grho[i], low[i]), high[i])
                sig[i + 2, R, :] = sig[i + 2, R, :] - step_s * gsig[i]
                return carry

            with scope("update"):
                lax.fori_loop(0, X, update, 0, unroll=4)
        with scope("zlin"):
            psq = zlin()
        if k == 0:
            with scope("yrimwait"):
                yrims_wait(0)
            for f, a in ((0, rho), (1, sig)):
                for s in range(2):
                    rim[f, s, 0, XI, :] = yrecv[0, s, f, 1]
                    rim[f, s, 1, XI, :] = yrecv[0, s, f, 0]
                    rim[f, s, 2, XI, :] = ysend[0, s, f, 0]
                    for sx in range(2):
                        rim[f, s, 1, 7 + sx * (X + 1):8 + sx * (X + 1), :] = crecv[0, sx, s, f:f + 1, :]
        else:
            with scope("yrimwait"):
                if k == 1:
                    yrims_wait(BOUNDS)
                yrims_wait(k)
            for s in range(2):
                for row, slot in ((0, 1), (1, 0), (2, 0)):
                    gr = (ysend[0, s, 0, 0] if row == 2 else yrecv[k, s, 0, slot])
                    gs = (ysend[0, s, 1, 0] if row == 2 else yrecv[k, s, 1, slot])
                    lo = (ysend[1, s, 0, 0] if row == 2 else yrecv[3, s, 0, slot])
                    hi = (ysend[1, s, 1, 0] if row == 2 else yrecv[3, s, 1, slot])
                    rim[0, s, row, XI, :] = jnp.minimum(jnp.maximum(rim[0, s, row, XI, :] - step_r * gr, lo), hi)
                    rim[1, s, row, XI, :] = rim[1, s, row, XI, :] - step_s * gs
                for sx in range(2):
                    at = slice(7 + sx * (X + 1), 8 + sx * (X + 1))
                    rim[0, s, 1, at, :] = jnp.minimum(jnp.maximum(
                        rim[0, s, 1, at, :] - step_r * crecv[k, sx, s, 0:1, :],
                        crecv[3, sx, s, 0:1, :]), crecv[3, sx, s, 1:2, :])
                    rim[1, s, 1, at, :] = rim[1, s, 1, at, :] - step_s * crecv[k, sx, s, 1:2, :]
        with scope("setrows"):
            lax.fori_loop(0, X, set_rows, 0, unroll=4)
            set_corners()
        with scope("edges"):
            edges()

        for s in range(2):
            def rimstep(q, carry):
                base = pl.multiple_of(q * 8, 8)
                def vec(f):
                    a1 = rim[f, s, 1, pl.ds(9 + base, 8), :] - rim[f, s, 1, pl.ds(7 + base, 8), :]
                    a2 = rim[f, s, 2 - 2 * s, pl.ds(8 + base, 8), :] - rim[f, s, 2 * s, pl.ds(8 + base, 8), :]
                    return a1, a2, dedge[pl.ds((2 * f + s) * X + base, 8), :]
                a1, a2, a3 = vec(0)
                b1, b2, b3 = vec(1)
                c1 = a2 * b3 - a3 * b2
                c3 = a1 * b2 - a2 * b1
                rim2[s, 0, pl.ds(base, 8), :] = b3 * c1 - b1 * c3
                rim2[s, 1, pl.ds(base, 8), :] = c3 * a1 - c1 * a3
                return carry
            with scope("rimstep"):
                lax.fori_loop(0, X // 8, rimstep, 0)

        def vectors(a, x, a3):
            a1 = a[x + 1, R, :] - a[x - 1, R, :]
            a2 = a[x, pl.ds(9, Y), :] - a[x, pl.ds(7, Y), :]
            return a1, a2, a3

        def edge(x):
            a1, a2, a3 = vectors(rho, x, slope(rho[x, R, :]))
            b1, b2, b3 = vectors(sig, x, slope(sig[x, R, :]))
            c2 = a3 * b1 - a1 * b3
            c3 = a1 * b2 - a2 * b1
            u1[x - 1] = b2 * c3 - b3 * c2
            v1[x - 1] = c2 * a3 - c3 * a2

        def pass1(i, acc):
            x = i + 2
            a1, a2, a3 = vectors(rho, x, da[i])
            b1, b2, b3 = vectors(sig, x, db[i])
            c1 = a2 * b3 - a3 * b2
            c2 = a3 * b1 - a1 * b3
            c3 = a1 * b2 - a2 * b1
            u1[i + 1] = b2 * c3 - b3 * c2
            v1[i + 1] = c2 * a3 - c3 * a2
            u2[i, R, :] = b3 * c1 - b1 * c3
            v2[i, R, :] = c3 * a1 - c1 * a3
            e3[i] = b1 * c2 - b2 * c1
            f3[i] = c1 * a2 - c2 * a1
            for s in range(2):
                at = pl.ds(7 + s * (Y + 1), 1)
                u2[i, at, :] = rim2[s, 0, pl.ds(i, 1), :]
                v2[i, at, :] = rim2[s, 1, pl.ds(i, 1), :]
            return acc + fold(c1 * c1 + c2 * c2 + c3 * c3)

        with scope("pass1"):
            csq = lax.fori_loop(2, X - 2, pass1, z8, unroll=4)
            csq = pass1(1, csq)
            csq = pass1(X - 2, csq)
        with scope("xrimwait"):
            if k == 1:
                xrims_wait(BOUNDS)
            xrims_wait(k)
        for s in range(2):
            pls = pl.ds(s * (X + 2), 2)
            if k == 0:
                rho[pls, R, :] = xrecv[0, s, 0]
                sig[pls, R, :] = xrecv[0, s, 1]
            else:
                rho[pls, R, :] = jnp.minimum(jnp.maximum(
                    rho[pls, R, :] - step_r * xrecv[k, s, 0], xrecv[3, s, 0]), xrecv[3, s, 1])
                sig[pls, R, :] = sig[pls, R, :] - step_s * xrecv[k, s, 1]
        rims_sent(k)
        if k == 0:
            with scope("rims3start"):
                rims_start(BOUNDS)
        with scope("edge"):
            edge(1)
            edge(X + 2)
            csq = pass1(0, csq)
            csq = pass1(X - 1, csq)

        with scope("pwwait"):
            if k == 0:
                a, b = pw_wait(0)
                before[...] = a
                zsum[...] = b + zown
            else:
                a, b = pw_wait(k)
                before[...] = before[...] - step_s * a
                zsum[...] = zsum[...] - (step_s * xscale) * (b + wg)
        start = xscale * (float(N) - i0) * before[...] + zsum[...]

        def pass2(i, carry):
            pref, back, acc, nrho, nsig = carry
            v = sig[i + 2, R, :]
            pref = pref + v
            rt = xscale * pref - t[i]
            adj_s = (v1[i] - v1[i + 2]) + (v2[i, pl.ds(7, Y), :] - v2[i, pl.ds(9, Y), :]) - f3[i]
            gs = xscale * back + (BETA / 16.0) * adj_s
            back = back - rt
            adj_r = (u1[i] - u1[i + 2]) + (u2[i, pl.ds(7, Y), :] - u2[i, pl.ds(9, Y), :]) - e3[i]
            gr = (zscale * zscale) * lin[i] - gp[i] + (BETA / 16.0) * adj_r
            grho[i] = gr
            gsig[i] = gs
            acc = acc + fold(rt * rt)
            nrho = nrho + fold(gr * gr)
            nsig = nsig + fold(gs * gs)
            if k < ITERS - 1:
                gather(0, 0, i, gr)
                gather(0, 1, i, gs)
            return pref, back, acc, nrho, nsig

        with scope("zadj"):
            for a in (e3, f3):
                a[...] = zslope(a[...].reshape(X * Y, Z)).reshape(X, Y, Z)
        with scope("pass2"):
            _, _, acc, nrho, nsig = lax.fori_loop(
                0, X, pass2, (before[...], start, z8, z8, z8), unroll=UNROLL2)
        local = (0.5 / cells) * (acc + psq + (BETA / 16.0) * csq)
        lane = lax.broadcasted_iota(jnp.int32, (1, Z), 1)

        def total(v):
            return jnp.sum(jnp.sum(v, axis=0, keepdims=True), axis=1, keepdims=True)

        row = jnp.where(lane < 1, total(nrho), jnp.where(lane < 2, total(nsig), total(local)))
        nsend[k, 0:1] = row
        nrecv[k, n - 1:n] = row
        with scope("nstart"):
            n_start(k)
        if k < ITERS - 1:
            with scope("rimstart"):
                corners(0)
                if k == 0:
                    rims_sent(BOUNDS)
                rims_start(k + 1)

            def weigh(i, carry):
                pg, wg = carry
                gs = gsig[i]
                return pg + gs, wg + (float(N) - i0 - i.astype(F32)) * gs

            with scope("weigh"):
                pg, wg = lax.fori_loop(0, X, weigh, (zero, zero), unroll=8)
                pwsend[0] = pg
                pwsend[1] = wg
                pw_start(k + 1)
        with scope("nwait"):
            tot = n_wait(k)
        steps = ETA * lax.rsqrt(tot / cells + EPSILON)
        step_r = jnp.broadcast_to(steps[0:1, 0:1], (1, Z))
        step_s = jnp.broadcast_to(steps[0:1, 1:2], (1, Z))
        stat[k:k + 1, :] = jnp.broadcast_to(tot[0:1, 2:3], (1, Z))
        if k == ITERS - 1:
            stat[ITERS:ITERS + 1, :] = step_r
            stat[ITERS + 1:ITERS + 2, :] = step_s


def finish(both, grad, lim, stat, rho_o, sig_o, obj_o, rho_b, sig_b, obj, sems):
    X, Y, Z = rho_b.shape
    R = pl.ds(8, Y)
    seen = stat[...]
    for k in range(ITERS):
        obj[k] = seen[k, 0]
    copies = [pltpu.make_async_copy(obj, obj_o, sems.at[0])]
    copies[0].start()
    step_r = stat[ITERS:ITERS + 1, :]
    step_s = stat[ITERS + 1:ITERS + 2, :]

    def move(i, carry):
        rho_b[i] = jnp.minimum(jnp.maximum(both[0, i + 2, R, :] - step_r * grad[0, i], lim[0, i]), lim[1, i])
        sig_b[i] = both[1, i + 2, R, :] - step_s * grad[1, i]
        return carry

    parts = 4
    for c in range(parts):
        lax.fori_loop(c * X // parts, (c + 1) * X // parts, move, 0, unroll=4)
        rows = pl.ds(c * X // parts, X // parts)
        for f, (a, b) in enumerate(((rho_b, rho_o), (sig_b, sig_o))):
            copies.append(pltpu.make_async_copy(a.at[rows], b.at[rows], sems.at[1 + 2 * c + f]))
            copies[-1].start()
    for c in copies:
        c.wait()


def local(density, slowness, pressure_obs, time_obs, zone_map, zone_low, zone_high):
    X, Y, Z = density.shape
    nx, ny = lax.axis_size("gx"), lax.axis_size("gy")
    assert Z <= 256
    V = pltpu.VMEM
    cube = (X, Y, Z)
    padded = (2, X + 4, Y + 16, Z)
    dma = pltpu.SemaphoreType.DMA
    anyspace = pl.BlockSpec(memory_space=pl.ANY)
    zones = zone_low.shape[0]
    scratch = [
        pltpu.SMEM((zones,), F32), pltpu.SMEM((zones,), F32),
        V(cube, F32), V(cube, F32),
        V(cube, jnp.int32), V(cube, F32), V(cube, F32),
        V((X + 2, Y, Z), F32), V((X + 2, Y, Z), F32), V((X, Y + 16, Z), F32), V((X, Y + 16, Z), F32),
        V(cube, F32), V(cube, F32), V(cube, F32), V(cube, F32), V((4 * X, Z), F32),
        V((2 * Z, 3 * Z), BF16), V((2 * Z, Z), BF16),
        V((2, 2, 3, X + 16, Z), F32), V((2, 2, X, Z), F32),
        V((2, 2, 2, 2, X, Z), F32), V((4, 2, 2, 2, X, Z), F32), V((4, 2, 2, 2, Y, Z), F32),
        V((2, 2, 2, 8, Z), F32), V((4, 2, 2, 8, Z), F32),
        V((2, Y, Z), F32), V((ITERS, nx - 1, Y, Z), F32), V((Y, Z), F32), V((Y, Z), F32),
        V((ITERS, 8, Z), F32), V((ITERS, nx * ny, Z), F32),
        dma((7,)), dma((2,)), dma((3, 2)), dma((2,)), dma((3, 2)),
        dma((2, 2)), dma((3, 2, 2)), dma((1,)), dma((2,)),
        dma((1,)), dma((2,)),
    ]
    inside = pl.BlockSpec(memory_space=pltpu.VMEM)
    state = pl.pallas_call(
        functools.partial(kernel, nx, ny),
        out_shape=(V(padded, F32), V((2,) + cube, F32), V((2,) + cube, F32), V((8, Z), F32)),
        in_specs=[pl.BlockSpec(memory_space=pltpu.HBM)] * 7,
        out_specs=(inside,) * 4,
        scratch_shapes=scratch,
        compiler_params=pltpu.CompilerParams(
            collective_id=0, has_side_effects=True, vmem_limit_bytes=48 * 1024 * 1024),
        name="inversion",
    )(zone_low, zone_high, density, slowness, pressure_obs, time_obs, zone_map)
    return pl.pallas_call(
        finish,
        out_shape=(
            jax.ShapeDtypeStruct(cube, F32),
            jax.ShapeDtypeStruct(cube, F32),
            jax.ShapeDtypeStruct((ITERS,), F32),
        ),
        in_specs=[inside] * 4,
        out_specs=(anyspace,) * 3,
        scratch_shapes=[V(cube, F32), V(cube, F32), pltpu.SMEM((ITERS,), F32), dma((9,))],
        compiler_params=pltpu.CompilerParams(vmem_limit_bytes=20 * 1024 * 1024),
        name="finish",
    )(*(pltpu.with_memory_space_constraint(a, pltpu.VMEM) for a in state))


def solution(mesh):
    cube = P("gx", "gy", None)
    return jax.shard_map(
        local,
        mesh=mesh,
        in_specs=(cube,) * 5 + (P(), P()),
        out_specs=(cube, cube, P()),
        check_vma=False,
    )
```

time: 47.5 us -> 43.9 us (0.924)
  Pallas kernels: 46.7 us -> 43.1 us
    pallas_call x1, Pallas kernels: 45.2 us -> 41.6 us  [local(): pl.pallas_call(functools.partial(kernel, nx, ny), out_shape=(V(padded, F3...]
where the time goes in v2:
time: 43.9 us; the launch traced here: 43.7 us
  Pallas kernels  43.1 us (98%)
  between operations  0.64 us (1%)
    pallas_call x1, Pallas kernels, local(): pl.pallas_call(functools.partial(kernel, nx, ny), out_shape=(V(padded, F3...  41.6 us
    pallas_call x1, Pallas kernels, local(): pl.pallas_call(finish, out_shape=(jax.ShapeDtypeStruct(cube, F32), jax.Sh...  1.51 us

profile of v2, /device:TPU:0, one launch (start us, length us, event | category | flops | bytes accessed | tf_op | source)
XLA Modules:
  0.0 43.7 jit_solution(3108476977815294205)
XLA Ops:
  0.6 41.6 %inversion.1 = (f32[2,68,48,128]{3,2,1,0:T(8,128)S(1)}, f32[2,64,32,128]{3,2,1,0:T(8,128)S(1)}, f32[2,64,32,128]{3,2,1,0:T(8,128)S(1)}, f32[8,128]{1,0:T(8,128)S(1)}) custom-call(f32[8]{0:T(128)} %zlow_h.1, f32[8]{0:T(128)} %zhigh_h.1, f32[64,32,128]{2,1,0:T(8,128)} %rho_h.1, f32[64,32,128]{2,1,0:T(8,128)} %sig_h.1, f32[64,32,128]{2,1,0:T(8,128)} %p_h.1, ...), custom_call_target="tpu_custom_call" | custom-call | tf_op jit(solution)/shard_map/inversion/pallas_call | solution.py:577
  42.2 1.5 %finish.1 = (f32[64,32,128]{2,1,0:T(8,128)}, f32[64,32,128]{2,1,0:T(8,128)}, f32[3]{0:T(128)}) custom-call(f32[2,68,48,128]{3,2,1,0:T(8,128)S(1)} %get-tuple-element.7.both, f32[2,64,32,128]{3,2,1,0:T(8,128)S(1)} %get-tuple-element.8.grad, f32[2,64,32,128]{3,2,1,0:T(8,128)S(1)} %get-tuple-element.9.lim, f32[8,128]{1,0:T(8,128)S(1)} %get-tuple-element.10.stat), custom_call_target="tpu_custom_call" | custom-call | tf_op jit(solution)/shard_map/finish/pallas_call | solution.py:587

commit v3 on v2

--- a/solution.py
+++ b/solution.py
@@ -18,6 +18,7 @@
 BOUNDS = 3
 BANK = (0, 1, 0, 2)
 UNROLL2 = 2
+GROUP = 8
 scope = jax.named_scope
 
 
@@ -32,7 +33,8 @@
     zlow_h, zhigh_h, rho_h, sig_h, p_h, t_h, zone_h,
     both, grad, lim, stat,
     zlow, zhigh, p, t, zone, gp, lin,
-    u1, v1, u2, v2, e3, f3, da, db, dedge, wts, ltab,
+    u1, v1, u2, v2, e3, f3, da, db, dg, miss, c1s, c2s, c3s, dedge, wts, ltab,
+    zsend, zyrecv, zxrecv, zcsend, zcrecv,
     rim, rim2, ysend, yrecv, xrecv, csend, crecv, pwsend, pwrecv, before, zsum, nsend, nrecv,
     insem, ys, yr, xs_, xr, cs, cr, ps, pr, ns, nr,
 ):
@@ -46,6 +48,8 @@
     cells = float(N * ny * Y * Z)
     zscale = 1.0 / math.sqrt(Z)
     xscale = 1.0 / math.sqrt(N)
+    gain = 16.0 / BETA
+    tscale = gain * xscale
     R = pl.ds(8, Y)
     XI = pl.ds(8, X)
     i0 = (mx * X).astype(F32)
@@ -76,44 +80,55 @@
     for dx, dy in pairs:
         pl.semaphore_signal(barrier, inc=1, device_id=other(dx, dy), device_id_type=MESH)
 
+    def blank(ref, at, value):
+        ref[at] = jnp.full(ref.shape[len(at):], value, ref.dtype)
+
     for s in range(2):
         @pl.when(jnp.logical_not(has[s][1]))
         def _():
-            for r in range(4):
-                yrecv[r, s] = jnp.zeros(yrecv.shape[2:], F32)
+            blank(zyrecv, (s,), -1)
+            for r in range(ITERS):
+                blank(yrecv, (r, s), 0.0)
 
         @pl.when(jnp.logical_not(has[s][0]))
         def _():
-            for r in range(4):
-                xrecv[r, s] = jnp.zeros(xrecv.shape[2:], F32)
+            blank(zxrecv, (s,), -1)
+            for r in range(ITERS):
+                blank(xrecv, (r, s), 0.0)
     for sx, sy in sides:
         @pl.when(jnp.logical_not(jnp.logical_and(has[sx][0], has[sy][1])))
         def _():
-            for r in range(4):
-                crecv[r, sx, sy] = jnp.zeros((8, Z), F32)
+            blank(zcrecv, (sx, sy), -1)
+            for r in range(ITERS):
+                blank(crecv, (r, sx, sy), 0.0)
 
     def ycopy(r, s):
         b = 1 if r == BOUNDS else 0
         return pltpu.make_async_remote_copy(
-            src_ref=ysend.at[b, s], dst_ref=yrecv.at[r, 1 - s],
-            send_sem=ys.at[s], recv_sem=yr.at[BANK[r], 1 - s],
+            src_ref=zsend.at[s] if b else ysend.at[0, s],
+            dst_ref=zyrecv.at[1 - s] if b else yrecv.at[r, 1 - s],
+            send_sem=ys.at[b, s], recv_sem=yr.at[BANK[r], 1 - s],
             device_id=(mx, my + (2 * s - 1)), device_id_type=MESH)
 
     def xcopy(r, s):
+        b = 1 if r == BOUNDS else 0
+        planes = pl.ds(s * (X - 2), 2)
         if r == 0:
             src = both.at[:, pl.ds(2 + s * (X - 2), 2), R]
         else:
-            src = (lim if r == BOUNDS else grad).at[:, pl.ds(s * (X - 2), 2)]
+            src = zone.at[planes] if b else grad.at[:, planes]
         return pltpu.make_async_remote_copy(
-            src_ref=src, dst_ref=xrecv.at[r, 1 - s],
-            send_sem=xs_.at[s], recv_sem=xr.at[BANK[r], 1 - s],
+            src_ref=src, dst_ref=zxrecv.at[1 - s] if b else xrecv.at[r, 1 - s],
+            send_sem=xs_.at[b, s], recv_sem=xr.at[BANK[r], 1 - s],
             device_id=(mx + (2 * s - 1), my), device_id_type=MESH)
 
     def ccopy(r, sx, sy):
         b = 1 if r == BOUNDS else 0
+        src = zcsend.at[sx, sy, pl.ds(0, 1)] if b else csend.at[sx, sy, pl.ds(0, 2)]
+        dst = zcrecv.at[1 - sx, 1 - sy, pl.ds(0, 1)] if b else crecv.at[r, 1 - sx, 1 - sy, pl.ds(0, 2)]
         return pltpu.make_async_remote_copy(
-            src_ref=csend.at[b, sx, sy, pl.ds(0, 2)], dst_ref=crecv.at[r, 1 - sx, 1 - sy, pl.ds(0, 2)],
-            send_sem=cs.at[sx, sy], recv_sem=cr.at[BANK[r], 1 - sx, 1 - sy],
+            src_ref=src, dst_ref=dst,
+            send_sem=cs.at[b, sx, sy], recv_sem=cr.at[BANK[r], 1 - sx, 1 - sy],
             device_id=(mx + (2 * sx - 1), my + (2 * sy - 1)), device_id_type=MESH)
 
     def rims_start(r):
@@ -213,10 +228,10 @@
         ysend[b, 1, f, 0, row, :] = v[Y - 1:Y]
         ysend[b, 1, f, 1, row, :] = v[Y - 2:Y - 1]
 
-    def corners(b):
+    def corners():
         for f in range(2):
             for sx, sy in sides:
-                csend[b, sx, sy, f:f + 1, :] = ysend[b, sy, f, 0, sx * (X - 1):sx * (X - 1) + 1, :]
+                csend[sx, sy, f:f + 1, :] = ysend[0, sy, f, 0, sx * (X - 1):sx * (X - 1) + 1, :]
 
     def slope(v):
         lane = lax.broadcasted_iota(jnp.int32, v.shape, 1)
@@ -248,7 +263,7 @@
         return carry
 
     lax.fori_loop(0, X, copy_rho, 0, unroll=4)
-    corners(0)
+    corners()
     with scope("barrier"):
         pl.semaphore_wait(barrier, n - 1)
     with scope("rims0start"):
@@ -258,23 +273,34 @@
     for c in loads[3:]:
         c.wait()
 
-    def bounds(x, carry):
-        ids = zone[x]
-        lo = jnp.zeros((Y, Z), F32)
-        hi = jnp.zeros((Y, Z), F32)
+    def limits(ids):
+        lo = jnp.zeros(ids.shape, F32)
+        hi = jnp.zeros(ids.shape, F32)
         for k in range(zlow.shape[0]):
             hit = ids == k
             lo = jnp.where(hit, zlow[k], lo)
             hi = jnp.where(hit, zhigh[k], hi)
+        return lo, hi
+
+    def bounds(x, carry):
+        ids = zone[x]
+        lo, hi = limits(ids)
+        row = pl.ds(x, 1)
+        for s in range(2):
+            for slot in range(2):
+                at = s * (Y - 1) + (1 - 2 * s) * slot
+                zsend[s, slot, row, :] = ids[at:at + 1]
         low[x] = lo
         high[x] = hi
+        t[x] = tscale * t[x]
         gather(1, 0, x, lo)
         gather(1, 1, x, hi)
         return carry
 
     with scope("bounds"):
         lax.fori_loop(0, X, bounds, 0, unroll=2)
-        corners(1)
+        for sx, sy in sides:
+            zcsend[sx, sy, 0:1, :] = zsend[sy, 0, sx * (X - 1):sx * (X - 1) + 1, :]
 
     ri = lax.broadcasted_iota(jnp.int32, (Z, Z), 0)
     ci = lax.broadcasted_iota(jnp.int32, (Z, Z), 1)
@@ -291,20 +317,26 @@
     with scope("pback"):
         v = p[...].reshape(X * Y, Z)
         out = jnp.dot(split(v), ltab[...], preferred_element_type=F32)
-        gp[...] = (out * zscale).reshape(X, Y, Z)
+        gp[...] = (out * (gain * zscale)).reshape(X, Y, Z)
+
+    def product(v, columns):
+        rows = v.shape[0] // 2
+        return jnp.concatenate([
+            jnp.dot(split(v[h * rows:(h + 1) * rows]), wts[:, columns], preferred_element_type=F32)
+            for h in range(2)], axis=0)
 
     def zslope(v):
-        return jnp.dot(split(v), wts[:, Z:2 * Z], preferred_element_type=F32)
-
-    def zlin():
-        v = rho[inner[0], R, :].reshape(X * Y, Z)
-        out = jnp.dot(split(v), wts[...], preferred_element_type=F32)
-        lin[...] = out[:, 0:Z].reshape(X, Y, Z)
+        return product(v, slice(Z, 2 * Z))
+
+    def zlin(v, columns):
+        out = product(v.reshape(X * Y, Z), slice(0, columns * Z))
+        lin[...] = (out[:, 0:Z] * (gain * zscale * zscale)).reshape(X, Y, Z)
         da[...] = out[:, Z:2 * Z].reshape(X, Y, Z)
-        rp = zscale * out[:, 2 * Z:3 * Z].reshape(X, Y, Z) - p[...]
-        v = sig[inner[0], R, :].reshape(X * Y, Z)
-        db[...] = zslope(v).reshape(X, Y, Z)
-        return fold((rp * rp).reshape(X * Y, Z))
+        return pressure(out[:, 2 * Z:3 * Z]) if columns > 2 else None
+
+    def pressure(v):
+        rp = zscale * v - p[...].reshape(X * Y, Z)
+        return fold(rp * rp)
 
     def edges():
         dedge[...] = slope(jnp.concatenate(
@@ -323,19 +355,23 @@
                     rim[f, sy, 1, 7 + sx * (X + 1):8 + sx * (X + 1), :])
 
     for k in range(ITERS):
-        if k > 0:
-            def update(i, carry):
-                rho[i + 2, R, :] = jnp.minimum(jnp.maximum(rho[i + 2, R, :] - step_r * grho[i], low[i]), high[i])
-                sig[i + 2, R, :] = sig[i + 2, R, :] - step_s * gsig[i]
-                return carry
-
+        late = k == ITERS - 1
+        if k == 0:
+            with scope("zlin"):
+                psq = zlin(rho[inner[0], R, :], 3)
+                db[...] = zslope(sig[inner[0], R, :].reshape(X * Y, Z)).reshape(X, Y, Z)
+        else:
             with scope("update"):
-                lax.fori_loop(0, X, update, 0, unroll=4)
-        with scope("zlin"):
-            psq = zlin()
+                v = jnp.minimum(jnp.maximum(rho[inner[0], R, :] - step_r * grho[...], low[...]), high[...])
+                rho[inner[0], R, :] = v
+                sig[inner[0], R, :] = sig[inner[0], R, :] - step_s * gsig[...]
+                db[...] = db[...] - step_s * dg[...]
+                psq = zlin(v, 3 if late else 2)
         if k == 0:
             with scope("yrimwait"):
                 yrims_wait(0)
+            with scope("rims3start"):
+                rims_start(BOUNDS)
             for f, a in ((0, rho), (1, sig)):
                 for s in range(2):
                     rim[f, s, 0, XI, :] = yrecv[0, s, f, 1]
@@ -345,8 +381,6 @@
                         rim[f, s, 1, 7 + sx * (X + 1):8 + sx * (X + 1), :] = crecv[0, sx, s, f:f + 1, :]
         else:
             with scope("yrimwait"):
-                if k == 1:
-                    yrims_wait(BOUNDS)
                 yrims_wait(k)
             for s in range(2):
                 for row, slot in ((0, 1), (1, 0), (2, 0)):
@@ -398,7 +432,7 @@
             u1[x - 1] = b2 * c3 - b3 * c2
             v1[x - 1] = c2 * a3 - c3 * a2
 
-        def pass1(i, acc):
+        def pass1(i, acc, turn=lambda v: v):
             x = i + 2
             a1, a2, a3 = vectors(rho, x, da[i])
             b1, b2, b3 = vectors(sig, x, db[i])
@@ -409,21 +443,35 @@
             v1[i + 1] = c2 * a3 - c3 * a2
             u2[i, R, :] = b3 * c1 - b1 * c3
             v2[i, R, :] = c3 * a1 - c1 * a3
-            e3[i] = b1 * c2 - b2 * c1
-            f3[i] = c1 * a2 - c2 * a1
+            e3[i] = turn(b1 * c2 - b2 * c1)
+            f3[i] = turn(c1 * a2 - c2 * a1)
             for s in range(2):
                 at = pl.ds(7 + s * (Y + 1), 1)
                 u2[i, at, :] = rim2[s, 0, pl.ds(i, 1), :]
                 v2[i, at, :] = rim2[s, 1, pl.ds(i, 1), :]
-            return acc + fold(c1 * c1 + c2 * c2 + c3 * c3)
+            if late:
+                return acc + fold(c1 * c1 + c2 * c2 + c3 * c3)
+            c1s[i] = c1
+            c2s[i] = c2
+            c3s[i] = c3
+            return acc
+
+        def zadj(i, m):
+            for a in (e3, f3):
+                a[i:i + m] = jnp.dot(
+                    split(a[i:i + m].reshape(m * Y, Z)), wts[:, Z:2 * Z],
+                    preferred_element_type=F32).reshape(m, Y, Z)
 
         with scope("pass1"):
-            csq = lax.fori_loop(2, X - 2, pass1, z8, unroll=4)
-            csq = pass1(1, csq)
-            csq = pass1(X - 2, csq)
+            csq = z8
+            done = 1
+            for i in range(1, X - 1):
+                csq = pass1(i, csq)
+                if i - done == GROUP or i == X - 2:
+                    last = i + 1 if i == X - 2 else i
+                    zadj(done, last - done)
+                    done = last
         with scope("xrimwait"):
-            if k == 1:
-                xrims_wait(BOUNDS)
             xrims_wait(k)
         for s in range(2):
             pls = pl.ds(s * (X + 2), 2)
@@ -435,39 +483,41 @@
                     rho[pls, R, :] - step_r * xrecv[k, s, 0], xrecv[3, s, 0]), xrecv[3, s, 1])
                 sig[pls, R, :] = sig[pls, R, :] - step_s * xrecv[k, s, 1]
         rims_sent(k)
-        if k == 0:
-            with scope("rims3start"):
-                rims_start(BOUNDS)
+        if k == 1:
+            rims_sent(BOUNDS)
         with scope("edge"):
             edge(1)
             edge(X + 2)
-            csq = pass1(0, csq)
-            csq = pass1(X - 1, csq)
+            csq = pass1(0, csq, slope)
+            csq = pass1(X - 1, csq, slope)
 
         with scope("pwwait"):
             if k == 0:
                 a, b = pw_wait(0)
-                before[...] = a
-                zsum[...] = b + zown
+                before[...] = (tscale * xscale) * a
+                zsum[...] = tscale * (b + zown)
             else:
                 a, b = pw_wait(k)
-                before[...] = before[...] - step_s * a
-                zsum[...] = zsum[...] - (step_s * xscale) * (b + wg)
-        start = xscale * (float(N) - i0) * before[...] + zsum[...]
+                before[...] = before[...] - (step_s * (tscale * xscale)) * a
+                zsum[...] = zsum[...] - (step_s * (tscale * xscale)) * (b + wg)
+        start = (float(N) - i0) * before[...] + zsum[...]
 
         def pass2(i, carry):
             pref, back, acc, nrho, nsig = carry
             v = sig[i + 2, R, :]
-            pref = pref + v
-            rt = xscale * pref - t[i]
+            pref = pref + (tscale * xscale) * v
+            rt = pref - t[i]
             adj_s = (v1[i] - v1[i + 2]) + (v2[i, pl.ds(7, Y), :] - v2[i, pl.ds(9, Y), :]) - f3[i]
-            gs = xscale * back + (BETA / 16.0) * adj_s
+            gs = back + adj_s
             back = back - rt
             adj_r = (u1[i] - u1[i + 2]) + (u2[i, pl.ds(7, Y), :] - u2[i, pl.ds(9, Y), :]) - e3[i]
-            gr = (zscale * zscale) * lin[i] - gp[i] + (BETA / 16.0) * adj_r
+            gr = lin[i] - gp[i] + adj_r
             grho[i] = gr
             gsig[i] = gs
-            acc = acc + fold(rt * rt)
+            if late:
+                acc = acc + fold(rt * rt)
+            else:
+                miss[i] = rt
             nrho = nrho + fold(gr * gr)
             nsig = nsig + fold(gs * gs)
             if k < ITERS - 1:
@@ -475,28 +525,31 @@
                 gather(0, 1, i, gs)
             return pref, back, acc, nrho, nsig
 
-        with scope("zadj"):
-            for a in (e3, f3):
-                a[...] = zslope(a[...].reshape(X * Y, Z)).reshape(X, Y, Z)
         with scope("pass2"):
-            _, _, acc, nrho, nsig = lax.fori_loop(
-                0, X, pass2, (before[...], start, z8, z8, z8), unroll=UNROLL2)
-        local = (0.5 / cells) * (acc + psq + (BETA / 16.0) * csq)
+            carry = (before[...], start, z8, z8, z8)
+            for i in range(X):
+                carry = pass2(i, carry)
+            _, _, acc, nrho, nsig = carry
+        def objective(acc, psq, csq):
+            return (0.5 / cells) * ((1.0 / (tscale * tscale)) * acc + psq + (BETA / 16.0) * csq)
+
         lane = lax.broadcasted_iota(jnp.int32, (1, Z), 1)
 
         def total(v):
             return jnp.sum(jnp.sum(v, axis=0, keepdims=True), axis=1, keepdims=True)
 
-        row = jnp.where(lane < 1, total(nrho), jnp.where(lane < 2, total(nsig), total(local)))
+        row = jnp.where(lane < 1, total(nrho), total(nsig))
+        if k > 0:
+            row = jnp.where(lane < 2, row, total(past))
+        if late:
+            row = jnp.where(lane < 3, row, total(objective(acc, psq, csq)))
         nsend[k, 0:1] = row
         nrecv[k, n - 1:n] = row
         with scope("nstart"):
             n_start(k)
         if k < ITERS - 1:
             with scope("rimstart"):
-                corners(0)
-                if k == 0:
-                    rims_sent(BOUNDS)
+                corners()
                 rims_start(k + 1)
 
             def weigh(i, carry):
@@ -509,13 +562,39 @@
                 pwsend[0] = pg
                 pwsend[1] = wg
                 pw_start(k + 1)
+
+            def squares(i, carry):
+                acc, csq = carry
+                c1, c2, c3, rt = c1s[i], c2s[i], c3s[i], miss[i]
+                return acc + fold(rt * rt), csq + fold(c1 * c1 + c2 * c2 + c3 * c3)
+
+            with scope("dg"):
+                dg[...] = zslope(gsig[...].reshape(X * Y, Z)).reshape(X, Y, Z)
+            with scope("squares"):
+                acc, csq = lax.fori_loop(0, X, squares, (z8, z8), unroll=4)
+            if k > 0:
+                with scope("psq"):
+                    psq = pressure(product(rho[inner[0], R, :].reshape(X * Y, Z), slice(2 * Z, 3 * Z)))
+            past = objective(acc, psq, csq)
+            if k == 0:
+                with scope("zonewait"):
+                    yrims_wait(BOUNDS)
+                    xrims_wait(BOUNDS)
+                for s in range(2):
+                    for slot in range(2):
+                        yrecv[BOUNDS, s, 0, slot], yrecv[BOUNDS, s, 1, slot] = limits(zyrecv[s, slot])
+                    xrecv[BOUNDS, s, 0], xrecv[BOUNDS, s, 1] = limits(zxrecv[s])
+                for sx, sy in sides:
+                    crecv[BOUNDS, sx, sy, 0:1, :], crecv[BOUNDS, sx, sy, 1:2, :] = limits(zcrecv[sx, sy, 0:1, :])
         with scope("nwait"):
             tot = n_wait(k)
-        steps = ETA * lax.rsqrt(tot / cells + EPSILON)
+        steps = (ETA / gain) * lax.rsqrt(tot / (gain * gain * cells) + EPSILON)
         step_r = jnp.broadcast_to(steps[0:1, 0:1], (1, Z))
         step_s = jnp.broadcast_to(steps[0:1, 1:2], (1, Z))
-        stat[k:k + 1, :] = jnp.broadcast_to(tot[0:1, 2:3], (1, Z))
-        if k == ITERS - 1:
+        if k > 0:
+            stat[k - 1:k, :] = jnp.broadcast_to(tot[0:1, 2:3], (1, Z))
+        if late:
+            stat[k:k + 1, :] = jnp.broadcast_to(tot[0:1, 3:4], (1, Z))
             stat[ITERS:ITERS + 1, :] = step_r
             stat[ITERS + 1:ITERS + 2, :] = step_s
 
@@ -562,15 +641,18 @@
         V(cube, F32), V(cube, F32),
         V(cube, jnp.int32), V(cube, F32), V(cube, F32),
         V((X + 2, Y, Z), F32), V((X + 2, Y, Z), F32), V((X, Y + 16, Z), F32), V((X, Y + 16, Z), F32),
-        V(cube, F32), V(cube, F32), V(cube, F32), V(cube, F32), V((4 * X, Z), F32),
+        V(cube, F32), V(cube, F32), V(cube, F32), V(cube, F32),
+        V(cube, F32), V(cube, F32), V(cube, F32), V(cube, F32), V(cube, F32), V((4 * X, Z), F32),
         V((2 * Z, 3 * Z), BF16), V((2 * Z, Z), BF16),
+        V((2, 2, X, Z), jnp.int32), V((2, 2, X, Z), jnp.int32), V((2, 2, Y, Z), jnp.int32),
+        V((2, 2, 8, Z), jnp.int32), V((2, 2, 8, Z), jnp.int32),
         V((2, 2, 3, X + 16, Z), F32), V((2, 2, X, Z), F32),
         V((2, 2, 2, 2, X, Z), F32), V((4, 2, 2, 2, X, Z), F32), V((4, 2, 2, 2, Y, Z), F32),
-        V((2, 2, 2, 8, Z), F32), V((4, 2, 2, 8, Z), F32),
+        V((2, 2, 8, Z), F32), V((4, 2, 2, 8, Z), F32),
         V((2, Y, Z), F32), V((ITERS, nx - 1, Y, Z), F32), V((Y, Z), F32), V((Y, Z), F32),
         V((ITERS, 8, Z), F32), V((ITERS, nx * ny, Z), F32),
-        dma((7,)), dma((2,)), dma((3, 2)), dma((2,)), dma((3, 2)),
-        dma((2, 2)), dma((3, 2, 2)), dma((1,)), dma((2,)),
+        dma((7,)), dma((2, 2)), dma((3, 2)), dma((2, 2)), dma((3, 2)),
+        dma((2, 2, 2)), dma((3, 2, 2)), dma((1,)), dma((2,)),
         dma((1,)), dma((2,)),
     ]
     inside = pl.BlockSpec(memory_space=pltpu.VMEM)

time: 43.9 us -> 39.1 us (0.89)
  Pallas kernels: 43.1 us -> 38.1 us
    pallas_call x1, Pallas kernels: 41.6 us -> 36.6 us  [local(): pl.pallas_call(functools.partial(kernel, nx, ny), out_shape=(V(padded, F3...]
where the time goes in v3:
time: 39.1 us; the launch traced here: 38.9 us
  Pallas kernels  38.1 us (97%)
  between operations  0.8 us (2%)
    pallas_call x1, Pallas kernels, local(): pl.pallas_call(functools.partial(kernel, nx, ny), out_shape=(V(padded, F3...  36.6 us
    pallas_call x1, Pallas kernels, local(): pl.pallas_call(finish, out_shape=(jax.ShapeDtypeStruct(cube, F32), jax.Sh...  1.51 us

profile of v3, /device:TPU:0, one launch (start us, length us, event | category | flops | bytes accessed | tf_op | source)
XLA Modules:
  0.0 38.9 jit_solution(4693976696504737451)
XLA Ops:
  0.6 36.6 %inversion.1 = (f32[2,68,48,128]{3,2,1,0:T(8,128)S(1)}, f32[2,64,32,128]{3,2,1,0:T(8,128)S(1)}, f32[2,64,32,128]{3,2,1,0:T(8,128)S(1)}, f32[8,128]{1,0:T(8,128)S(1)}) custom-call(f32[8]{0:T(128)} %zlow_h.1, f32[8]{0:T(128)} %zhigh_h.1, f32[64,32,128]{2,1,0:T(8,128)} %rho_h.1, f32[64,32,128]{2,1,0:T(8,128)} %sig_h.1, f32[64,32,128]{2,1,0:T(8,128)} %p_h.1, ...), custom_call_target="tpu_custom_call" | custom-call | tf_op jit(solution)/shard_map/inversion/pallas_call | solution.py:659
  37.2 1.5 %finish.1 = (f32[64,32,128]{2,1,0:T(8,128)}, f32[64,32,128]{2,1,0:T(8,128)}, f32[3]{0:T(128)}) custom-call(f32[2,68,48,128]{3,2,1,0:T(8,128)S(1)} %get-tuple-element.7.both, f32[2,64,32,128]{3,2,1,0:T(8,128)S(1)} %get-tuple-element.8.grad, f32[2,64,32,128]{3,2,1,0:T(8,128)S(1)} %get-tuple-element.9.lim, f32[8,128]{1,0:T(8,128)S(1)} %get-tuple-element.10.stat), custom_call_target="tpu_custom_call" | custom-call | tf_op jit(solution)/shard_map/finish/pallas_call | solution.py:669

commit v4 on v3

--- a/solution.py
+++ b/solution.py
@@ -64,7 +64,7 @@
         pltpu.make_async_copy(zlow_h, zlow, insem.at[5]),
         pltpu.make_async_copy(zhigh_h, zhigh, insem.at[6]),
     ]
-    for c in loads:
+    for c in loads[:3]:
         c.start()
     barrier = pltpu.get_barrier_semaphore()
 
@@ -77,8 +77,19 @@
         return tx, ty
 
     pairs = [(dx, dy) for dx in range(nx) for dy in range(ny)][1:]
-    for dx, dy in pairs:
+    lines = [(dx, dy) for dx, dy in pairs if dx == 0 or dy == 0]
+    for dx, dy in lines:
         pl.semaphore_signal(barrier, inc=1, device_id=other(dx, dy), device_id_type=MESH)
+    count = len(lines)
+    for sx, sy in sides:
+        diagonal = jnp.logical_and(has[sx][0], has[sy][1])
+        count = count + diagonal.astype(jnp.int32)
+
+        @pl.when(diagonal)
+        def _():
+            pl.semaphore_signal(
+                barrier, inc=1, device_id=(mx + (2 * sx - 1), my + (2 * sy - 1)), device_id_type=MESH)
+
 
     def blank(ref, at, value):
         ref[at] = jnp.full(ref.shape[len(at):], value, ref.dtype)
@@ -244,6 +255,8 @@
     with scope("load02"):
         loads[0].wait()
         loads[2].wait()
+        for c in loads[3:]:
+            c.start()
 
     def sums(x, carry):
         a, b, c = carry
@@ -265,7 +278,7 @@
     lax.fori_loop(0, X, copy_rho, 0, unroll=4)
     corners()
     with scope("barrier"):
-        pl.semaphore_wait(barrier, n - 1)
+        pl.semaphore_wait(barrier, count)
     with scope("rims0start"):
         rims_start(0)
         pw_start(0)
@@ -342,11 +355,10 @@
         dedge[...] = slope(jnp.concatenate(
             [rim[f, s, 1, XI, :] for f in range(2) for s in range(2)], axis=0))
 
-    def set_rows(x, carry):
+    def set_rows(x):
         for f, a in ((0, rho), (1, sig)):
             for s in range(2):
-                a[x + 2, pl.ds(7 + s * (Y + 1), 1), :] = rim[f, s, 1, pl.ds(8 + x, 1), :]
-        return carry
+                a[x + 2, 7 + s * (Y + 1):8 + s * (Y + 1), :] = rim[f, s, 1, 8 + x:9 + x, :]
 
     def set_corners():
         for f, a in ((0, rho), (1, sig)):
@@ -397,27 +409,28 @@
                         crecv[3, sx, s, 0:1, :]), crecv[3, sx, s, 1:2, :])
                     rim[1, s, 1, at, :] = rim[1, s, 1, at, :] - step_s * crecv[k, sx, s, 1:2, :]
         with scope("setrows"):
-            lax.fori_loop(0, X, set_rows, 0, unroll=4)
+            for x in range(X):
+                set_rows(x)
             set_corners()
         with scope("edges"):
             edges()
 
         for s in range(2):
-            def rimstep(q, carry):
-                base = pl.multiple_of(q * 8, 8)
+            def rimstep(base):
                 def vec(f):
-                    a1 = rim[f, s, 1, pl.ds(9 + base, 8), :] - rim[f, s, 1, pl.ds(7 + base, 8), :]
-                    a2 = rim[f, s, 2 - 2 * s, pl.ds(8 + base, 8), :] - rim[f, s, 2 * s, pl.ds(8 + base, 8), :]
-                    return a1, a2, dedge[pl.ds((2 * f + s) * X + base, 8), :]
+                    a1 = rim[f, s, 1, 9 + base:17 + base, :] - rim[f, s, 1, 7 + base:15 + base, :]
+                    a2 = rim[f, s, 2 - 2 * s, 8 + base:16 + base, :] - rim[f, s, 2 * s, 8 + base:16 + base, :]
+                    at = (2 * f + s) * X + base
+                    return a1, a2, dedge[at:at + 8, :]
                 a1, a2, a3 = vec(0)
                 b1, b2, b3 = vec(1)
                 c1 = a2 * b3 - a3 * b2
                 c3 = a1 * b2 - a2 * b1
-                rim2[s, 0, pl.ds(base, 8), :] = b3 * c1 - b1 * c3
-                rim2[s, 1, pl.ds(base, 8), :] = c3 * a1 - c1 * a3
-                return carry
-            with scope("rimstep"):
-                lax.fori_loop(0, X // 8, rimstep, 0)
+                rim2[s, 0, base:base + 8, :] = b3 * c1 - b1 * c3
+                rim2[s, 1, base:base + 8, :] = c3 * a1 - c1 * a3
+
+            for base in range(0, X, 8):
+                rimstep(base)
 
         def vectors(a, x, a3):
             a1 = a[x + 1, R, :] - a[x - 1, R, :]

time: 39.1 us -> 37.6 us (0.962)
  Pallas kernels: 38.1 us -> 36.6 us
    pallas_call x1, Pallas kernels: 36.6 us -> 35.1 us  [local(): pl.pallas_call(functools.partial(kernel, nx, ny), out_shape=(V(padded, F3...]
where the time goes in v4:
time: 37.6 us; the launch traced here: 37.4 us
  Pallas kernels  36.6 us (97%)
  between operations  0.8 us (2%)
    pallas_call x1, Pallas kernels, local(): pl.pallas_call(functools.partial(kernel, nx, ny), out_shape=(V(padded, F3...  35.1 us
    pallas_call x1, Pallas kernels, local(): pl.pallas_call(finish, out_shape=(jax.ShapeDtypeStruct(cube, F32), jax.Sh...  1.51 us

profile of v4, /device:TPU:0, one launch (start us, length us, event | category | flops | bytes accessed | tf_op | source)
XLA Modules:
  0.0 37.4 jit_solution(15284512745586438582)
XLA Ops:
  0.6 35.1 %inversion.1 = (f32[2,68,48,128]{3,2,1,0:T(8,128)S(1)}, f32[2,64,32,128]{3,2,1,0:T(8,128)S(1)}, f32[2,64,32,128]{3,2,1,0:T(8,128)S(1)}, f32[8,128]{1,0:T(8,128)S(1)}) custom-call(f32[8]{0:T(128)} %zlow_h.1, f32[8]{0:T(128)} %zhigh_h.1, f32[64,32,128]{2,1,0:T(8,128)} %rho_h.1, f32[64,32,128]{2,1,0:T(8,128)} %sig_h.1, f32[64,32,128]{2,1,0:T(8,128)} %p_h.1, ...), custom_call_target="tpu_custom_call" | custom-call | tf_op jit(solution)/shard_map/inversion/pallas_call | solution.py:672
  35.8 1.5 %finish.1 = (f32[64,32,128]{2,1,0:T(8,128)}, f32[64,32,128]{2,1,0:T(8,128)}, f32[3]{0:T(128)}) custom-call(f32[2,68,48,128]{3,2,1,0:T(8,128)S(1)} %get-tuple-element.7.both, f32[2,64,32,128]{3,2,1,0:T(8,128)S(1)} %get-tuple-element.8.grad, f32[2,64,32,128]{3,2,1,0:T(8,128)S(1)} %get-tuple-element.9.lim, f32[8,128]{1,0:T(8,128)S(1)} %get-tuple-element.10.stat), custom_call_target="tpu_custom_call" | custom-call | tf_op jit(solution)/shard_map/finish/pallas_call | solution.py:682
